TPU v7x, 128 devices: a whole 4x4x4 slice. The times are simulated.
128 devices in a mesh: src: 16 (over z, x), rcv: 8 (over y, core).
Axes of the slice: x: 4, y: 4, z: 4, core: 2. Of those that a mesh axis runs over, the one named last changes fastest.
Arguments:
- traces: bfloat16 [2, 2, 2048, 2048], P(None, None, 'src', 'rcv'), may hold values from -8 to 8
- wavelet: float32 [2, 2], replicated, may hold values from -0.3 to 0.3
Outputs:
- coeffs: float32 [2, 2, 2048, 2048], P(None, None, 'src', 'rcv')
- norms: float32 [2, 2], replicated
All inputs are finite; a program needn't handle non-finite values.
Results may differ from a plain program's by a relative error of at most 0.006.
Values may be sent and summed in bfloat16 or wider, within the bound.
A program may use at most 128 MiB of HBM per device.

v0:
```python
import math

import jax
import jax.numpy as jnp
from jax import lax
from jax.sharding import Mesh
from jax.sharding import PartitionSpec as P

ITERS = 2
SRC = ("src_0", "src_1")
RCV = ("rcv_0", "rcv_1")
SRC_RCV = ("src_0", "src_1", "rcv_0", "rcv_1")


step_length = 0.4
shrink_fraction = 0.2


def laid_out(tiles, dim):
    shape = list(tiles.shape[1:])
    shape[dim] *= tiles.shape[0]
    return jnp.moveaxis(tiles, 0, dim).reshape(shape)


def copy_for_each(x, axis):
    copies = jnp.broadcast_to(x, (lax.axis_size(axis), *x.shape))
    return lax.all_to_all(copies, axis, split_axis=0, concat_axis=0, tiled=True)


def gathered_copies(x, axis, dim):
    return laid_out(copy_for_each(x, axis), dim)


def all_in_one(x, axis):
    leaves = jax.tree.leaves(x)
    order = sorted(range(len(leaves)), key=lambda k: -leaves[k].size)
    width = (1, *leaves[order[0]].shape)[-1]
    lines = [
        jnp.pad(leaves[k].reshape(-1), (0, -leaves[k].size % width)).reshape(-1, width)
        for k in order
    ]
    both, at, found = (lax.all_gather(jnp.concatenate(lines), axis), 0, {})
    for k, line in zip(order, lines):
        share = both[:, at : at + len(line)].reshape(len(both), -1)
        found[k] = share[:, : leaves[k].size].reshape(-1, *leaves[k].shape)
        at += len(line)
    numbers = iter(range(len(leaves)))
    return jax.tree.map(lambda _: found[next(numbers)], x)


def once_a_type(x, axis):
    leaves, found = (jax.tree.leaves(x), {})
    for first, a in enumerate(leaves):
        if first not in found:
            alike = [k for k, b in enumerate(leaves) if b.dtype == a.dtype]
            got = (
                all_in_one([leaves[k] for k in alike], axis)
                if len(alike) > 1
                else [lax.all_gather(a, axis)]
            )
            for k, b in zip(alike, got):
                found[k] = b
    numbers = iter(range(len(leaves)))
    return jax.tree.map(lambda _: found[next(numbers)], x)


def joined_all(x, axes, combine):
    for axis in axes:
        pieces = once_a_type(x, axis)
        x = jax.tree.map(lambda part: part[0], pieces)
        for k in range(1, lax.axis_size(axis)):
            x = combine(x, jax.tree.map(lambda part: part[k], pieces))
    return x


def table_block(offset, height, second, breadth, length, direction):
    left_index = offset + jnp.arange(height, dtype=jnp.int32)
    right_index = second + jnp.arange(breadth, dtype=jnp.int32)
    phase = left_index[:, None] * right_index[None, :] % length
    angle = phase.astype(jnp.float32) * (2.0 * math.pi / length)
    scale = 1.0 / math.sqrt(length)
    return jnp.stack([jnp.cos(angle) * scale, direction * (jnp.sin(angle) * scale)]).astype(
        jnp.bfloat16
    )


def complex_product(left_side, right_side, pattern, left_table, right_table):
    left_re = left_side[0] if left_table else left_side[:, 0]
    left_im = left_side[1] if left_table else left_side[:, 1]
    right_re = right_side[0] if right_table else right_side[:, 0]
    right_im = right_side[1] if right_table else right_side[:, 1]

    def single(first_op, second_op):
        return jnp.einsum(pattern, first_op, second_op, preferred_element_type=jnp.float32)

    real_part = single(left_re, right_re) - single(left_im, right_im)
    imag_part = single(left_re, right_im) + single(left_im, right_re)
    return jnp.stack([real_part, imag_part], axis=1)


def complex_scale(real_part, imag_part, values):
    return jnp.stack(
        [
            real_part * values[:, 0] - imag_part * values[:, 1],
            real_part * values[:, 1] + imag_part * values[:, 0],
        ],
        axis=1,
    )


def combine_stats(first_pair, second_pair):
    return (jnp.maximum(first_pair[0], second_pair[0]), first_pair[1] + second_pair[1])


def per_device(traces, wavelet):
    row_count = traces.shape[2]
    col_count = traces.shape[3]
    extent = row_count * lax.axis_size(SRC)
    row_anchor = lax.axis_index(SRC) * row_count
    col_anchor = lax.axis_index(RCV) * col_count
    root_scale = 1.0 / math.sqrt(extent)
    wave_re = (wavelet[:, 0] * root_scale)[:, None, None]
    wave_im = (wavelet[:, 1] * root_scale)[:, None, None]
    forward_cols = table_block(0, extent, col_anchor, col_count, extent, -1.0)
    forward_rows = table_block(row_anchor, row_count, 0, extent, extent, -1.0)
    inverse_cols = table_block(0, extent, col_anchor, col_count, extent, 1.0)
    inverse_rows = table_block(row_anchor, row_count, 0, extent, extent, 1.0)
    coeffs = jnp.zeros(traces.shape, jnp.float32)
    columns_all = lax.all_gather(traces, SRC, axis=2, tiled=True)
    traces_f = traces.astype(jnp.float32)

    def column_section(table, portion):
        return complex_product(table, portion, "mn,fnc->fmc", True, False)

    def paired(first_op, second_op):
        return jnp.einsum("fmr,fkr->fmk", first_op, second_op, preferred_element_type=jnp.float32)

    norm_list = []
    for iteration in range(ITERS):
        if iteration == 0:
            misfit = traces_f
        else:
            coeff_half = coeffs.astype(jnp.bfloat16)
            halfway = column_section(
                inverse_rows, lax.all_gather(coeff_half, SRC, axis=2, tiled=True)
            ).astype(jnp.bfloat16)
            model = complex_product(
                gathered_copies(halfway, RCV, 3), inverse_cols, "fmn,nc->fmc", False, True
            ).astype(jnp.bfloat16)
            product = complex_product(
                gathered_copies(model, RCV, 3), columns_all, "fmn,fnc->fmc", False, False
            )
            misfit = traces_f - model.astype(jnp.float32) + complex_scale(wave_re, wave_im, product)
        local_squares = jnp.sum(misfit * misfit, axis=(1, 2, 3))
        misfit_half = misfit.astype(jnp.bfloat16)
        misfit_re = misfit_half[:, 0]
        misfit_im = misfit_half[:, 1]
        column_re = columns_all[:, 0]
        column_im = columns_all[:, 1]
        back_re = paired(misfit_re, column_re) + paired(misfit_im, column_re * 0 + column_im)
        back_im = paired(misfit_im, column_re) - paired(misfit_re, column_im)
        scaled = complex_scale(wave_re, -wave_im, jnp.stack([back_re, back_im], axis=1))
        embedded = lax.dynamic_update_slice(
            jnp.zeros_like(scaled), misfit_half.astype(jnp.float32), (0, 0, 0, col_anchor)
        )
        gradient_rows = lax.psum(embedded - scaled, RCV)
        halfway = complex_product(
            gradient_rows.astype(jnp.bfloat16), forward_cols, "fmn,nc->fmc", False, True
        ).astype(jnp.bfloat16)
        spectrum = column_section(forward_rows, lax.all_gather(halfway, SRC, axis=2, tiled=True))
        trial = coeffs + step_length * spectrum
        magnitude = jnp.sqrt(trial[:, 0] * trial[:, 0] + trial[:, 1] * trial[:, 1])
        local_peak = jnp.max(magnitude, axis=(1, 2))
        global_peak, total_squares = joined_all((local_peak, local_squares), SRC_RCV, combine_stats)
        norm_list.append(jnp.sqrt(total_squares))
        level = shrink_fraction * global_peak[:, None, None]
        factor = jnp.maximum(1.0 - level / jnp.maximum(magnitude, level), 0.0)
        coeffs = trial * factor[:, None]
    return (coeffs, jnp.stack(norm_list))


def solution(mesh):
    split = Mesh(mesh.devices.reshape(4, 4, 4, 2), ("src_0", "src_1", "rcv_0", "rcv_1"))
    return jax.shard_map(
        per_device,
        mesh=split,
        in_specs=(P(None, None, SRC, RCV), P()),
        out_specs=(P(None, None, SRC, RCV), P()),
        check_vma=False,
    )
```

profile of v0, /device:TPU:1, one launch (start us, length us, event | category | flops | bytes accessed | tf_op | source)
XLA Modules:
  0.0 641.6 jit_solution(3735553232752024656)
XLA Ops:
  7.2 1.7 copy.19
  9.0 1.0 multiply_reduce_fusion.2
  10.0 2.5 broadcast.426.clone
  12.5 0.9 fusion.79
  13.3 51.9 %all-gather.21.cloned.1.call-done = bf16[2,2,2048,256]{3,2,0,1:T(8,128)(2,1)} async-done(((bf16[2,2,128,256]{3,2,0,1:T(8,128)(2,1)}), bf16[2,2,2048,256]{3,2,0,1:T(8,128)(2,1)}) %all-gather.21.cloned.1.call-update) | async-done | bytes 4194320 | tf_op jit(solution)/shard_map/all_gather | solution.py:129
  65.3 2.5 fusion.78
  68.1 0.8 fusion.77
  68.9 0.8 fusion
  69.7 1.0 subtract_bitcast_fusion.1
  70.7 5.0 maximum_subtract_fusion
  75.7 56.3 %all-reduce.2 = bf16[2,2,128,2048]{3,2,0,1:T(8,128)(2,1)S(1)} all-reduce(f32[2,2,128,2048]{3,2,0,1:T(8,128)} %maximum_subtract_fusion), channel_id=1, replica_groups=mesh['src_0'=4,'src_1'=4,'rcv_0'=4,'rcv_1'=2] {'rcv_0','rcv_1'}, use_global_device_ids=true, to_apply=%region_0.1 | all-reduce | flops 1048576 | bytes 6291456 | tf_op jit(solution)/shard_map/psum | solution.py:166
  132.0 7.9 %fusion.62 = f32[2,128,256]{2,1,0:T(8,128)S(1)} fusion(s32[256]{0:T(256)S(1)} %iota_add_fusion, bf16[2,2,128,2048]{3,2,0,1:T(8,128)(2,1)S(1)} %all-reduce.2), kind=kOutput, calls=%fused_computation.104 | convolution fusion | flops 276824064 | bytes 1311744 | tf_op jit(solution)/shard_map/fmn,nc->fmc/dot_general | solution.py:94
  139.9 8.5 %fusion.67 = f32[2,128,256]{2,1,0:T(8,128)S(1)} fusion(s32[256]{0:T(256)S(1)} %iota_add_fusion, bf16[2,2,128,2048]{3,2,0,1:T(8,128)(2,1)S(1)} %all-reduce.2), kind=kOutput, calls=%fused_computation.106 | convolution fusion | flops 276824064 | bytes 1311744 | tf_op jit(solution)/shard_map/fmn,nc->fmc/dot_general | solution.py:94
  148.4 8.1 %fusion.44 = bf16[2,1,128,256]{3,2,0,1:T(8,128)(2,1)S(1)} fusion(f32[2,128,256]{2,1,0:T(8,128)S(1)} %fusion.62, s32[256]{0:T(256)S(1)} %iota_add_fusion, bf16[2,2,128,2048]{3,2,0,1:T(8,128)(2,1)S(1)} %all-reduce.2), kind=kOutput, calls=%fused_computation.80 | convolution fusion | flops 276955136 | bytes 1442816 | tf_op jit(solution)/shard_map/fmn,nc->fmc/dot_general | solution.py:94
  156.5 7.9 %fusion.43 = bf16[2,1,128,256]{3,2,0,1:T(8,128)(2,1)S(1)} fusion(f32[2,128,256]{2,1,0:T(8,128)S(1)} %fusion.67, s32[256]{0:T(256)S(1)} %iota_add_fusion, bf16[2,2,128,2048]{3,2,0,1:T(8,128)(2,1)S(1)} %all-reduce.2), kind=kOutput, calls=%fused_computation.79 | convolution fusion | flops 276955136 | bytes 1442816 | tf_op jit(solution)/shard_map/fmn,nc->fmc/dot_general | solution.py:94
  164.4 0.7 pad_maximum_fusion.1
  165.4 51.3 %all-gather.23.cloned.1.call-done = bf16[2,2,2048,256]{3,2,0,1:T(8,128)(2,1)} async-done(((bf16[2,2,128,256]{3,2,0,1:T(8,128)(2,1)}), bf16[2,2,2048,256]{3,2,0,1:T(8,128)(2,1)}) %all-gather.23.cloned.1.call-update) | async-done | bytes 4194320 | tf_op jit(solution)/shard_map/all_gather | solution.py:170
  216.7 6.0 fusion.8
  222.8 4.3 fusion.7
  227.1 4.7 fusion.26
  231.8 4.3 fusion.28
  236.3 7.6 %all-gather.8 = f32[4,2,2]{2,1,0:T(2,128)S(1)} all-gather(f32[1,2,2]{2,1,0:T(2,128)S(1)} %maximum_bitcast_fusion.1), channel_id=2, replica_groups=mesh['src_0'=4,'src_1'=4,'rcv_0'=4,'rcv_1'=2] {'src_0'}, dimensions={0}, use_global_device_ids=true | all-gather | bytes 80 | tf_op jit(solution)/shard_map/all_gather | solution.py:42
  244.0 5.9 all-gather.9
  249.9 7.8 %all-gather.10 = f32[4,2,2]{2,1,0:T(2,128)S(1)} all-gather(f32[1,2,2]{2,1,0:T(2,128)S(1)} %maximum_bitcast_fusion.3), channel_id=4, replica_groups=mesh['src_0'=4,'src_1'=4,'rcv_0'=4,'rcv_1'=2] {'rcv_0'}, dimensions={0}, use_global_device_ids=true | all-gather | bytes 80 | tf_op jit(solution)/shard_map/all_gather | solution.py:42
  257.7 8.2 %all-gather.11 = f32[2,2,2]{2,1,0:T(2,128)S(1)} all-gather(f32[1,2,2]{2,1,0:T(2,128)S(1)} %maximum_bitcast_fusion.4), channel_id=5, replica_groups=mesh['src_0'=4,'src_1'=4,'rcv_0'=4,'rcv_1'=2] {'rcv_1'}, dimensions={0}, use_global_device_ids=true | all-gather | bytes 48 | tf_op jit(solution)/shard_map/all_gather | solution.py:42
  266.0 0.8 multiply_convert_fusion.6
  267.1 50.2 %all-gather.25.cloned.1.call-done = bf16[2,2,2048,256]{2,3,0,1:T(8,128)(2,1)} async-done(((bf16[2,2,128,256]{2,3,0,1:T(8,128)(2,1)}), bf16[2,2,2048,256]{2,3,0,1:T(8,128)(2,1)}) %all-gather.25.cloned.1.call-update) | async-done | bytes 4194320 | tf_op jit(solution)/shard_map/all_gather | solution.py:145
  317.3 6.1 fusion.12
  323.4 4.4 fusion.11
  327.8 4.8 fusion.37
  332.6 4.4 fusion.38
  337.4 32.3 %all_to_all.10 = bf16[8,2,2,128,256]{4,3,1,2,0:T(8,128)(2,1)S(1)} all-to-all(bf16[8,2,2,128,256]{4,3,1,2,0:T(8,128)(2,1)S(1)} %broadcast_in_dim.4), channel_id=1, replica_groups=mesh['src_0'=4,'src_1'=4,'rcv_0'=4,'rcv_1'=2] {'rcv_0','rcv_1'}, dimensions={0} | all-to-all | bytes 4194304 | tf_op jit(solution)/shard_map/all_to_all | solution.py:27
  370.0 7.9 %fusion.59 = f32[2,128,256]{2,1,0:T(8,128)S(1)} fusion(s32[256]{0:T(256)S(1)} %iota_add_fusion, bf16[2,2,128,2048]{3,2,0,1:T(8,128)(2,1)S(1)} %bitcast.296), kind=kOutput, calls=%fused_computation.103 | convolution fusion | flops 276824064 | bytes 1311744 | tf_op jit(solution)/shard_map/fmn,nc->fmc/dot_general | solution.py:94
  377.9 8.1 %fusion.70 = f32[2,128,256]{2,1,0:T(8,128)S(1)} fusion(s32[256]{0:T(256)S(1)} %iota_add_fusion, bf16[2,2,128,2048]{3,2,0,1:T(8,128)(2,1)S(1)} %bitcast.297), kind=kOutput, calls=%fused_computation.107 | convolution fusion | flops 276824064 | bytes 1311744 | tf_op jit(solution)/shard_map/fmn,nc->fmc/dot_general | solution.py:94
  386.0 8.4 %fusion.42 = bf16[2,1,128,256]{3,2,0,1:T(8,128)(2,1)S(1)} fusion(f32[2,128,256]{2,1,0:T(8,128)S(1)} %fusion.59, s32[256]{0:T(256)S(1)} %iota_add_fusion, bf16[2,2,128,2048]{3,2,0,1:T(8,128)(2,1)S(1)} %bitcast.298), kind=kOutput, calls=%fused_computation.78 | convolution fusion | flops 276955136 | bytes 1442816 | tf_op jit(solution)/shard_map/fmn,nc->fmc/dot_general | solution.py:94
  394.4 7.9 %fusion.41 = bf16[2,1,128,256]{3,2,0,1:T(8,128)(2,1)S(1)} fusion(f32[2,128,256]{2,1,0:T(8,128)S(1)} %fusion.70, s32[256]{0:T(256)S(1)} %iota_add_fusion, bf16[2,2,128,2048]{3,2,0,1:T(8,128)(2,1)S(1)} %bitcast.299), kind=kOutput, calls=%fused_computation.77 | convolution fusion | flops 276955136 | bytes 1442816 | tf_op jit(solution)/shard_map/fmn,nc->fmc/dot_general | solution.py:94
  402.6 29.7 %all_to_all.11 = bf16[8,2,2,128,256]{4,3,1,2,0:T(8,128)(2,1)S(1)} all-to-all(bf16[8,2,2,128,256]{4,3,1,2,0:T(8,128)(2,1)S(1)} %broadcast_in_dim.5), channel_id=1, replica_groups=mesh['src_0'=4,'src_1'=4,'rcv_0'=4,'rcv_1'=2] {'rcv_0','rcv_1'}, dimensions={0} | all-to-all | bytes 4194304 | tf_op jit(solution)/shard_map/all_to_all | solution.py:27
  432.5 1.9 copy-done.1
  434.9 0.5 fusion.45
  435.3 0.5 convolution_add_fusion.2
  435.8 0.5 subtract_bitcast_fusion.2
  436.3 0.5 broadcast.426
  437.0 0.8 fusion.76
  437.9 0.8 fusion.75
  438.7 0.8 convolution_add_fusion
  439.5 0.9 subtract_bitcast_fusion
  440.5 2.7 maximum_subtract_fusion.1
  443.2 56.3 %all-reduce.3 = bf16[2,2,128,2048]{3,2,0,1:T(8,128)(2,1)S(1)} all-reduce(f32[2,2,128,2048]{3,2,0,1:T(8,128)} %maximum_subtract_fusion.1), channel_id=1, replica_groups=mesh['src_0'=4,'src_1'=4,'rcv_0'=4,'rcv_1'=2] {'rcv_0','rcv_1'}, use_global_device_ids=true, to_apply=%region_3.4 | all-reduce | flops 1048576 | bytes 6291456 | tf_op jit(solution)/shard_map/psum | solution.py:166
  499.5 7.9 %fusion.56 = f32[2,128,256]{2,1,0:T(8,128)S(1)} fusion(s32[256]{0:T(256)S(1)} %iota_add_fusion, bf16[2,2,128,2048]{3,2,0,1:T(8,128)(2,1)S(1)} %all-reduce.3), kind=kOutput, calls=%fused_computation.102 | convolution fusion | flops 276824064 | bytes 1311744 | tf_op jit(solution)/shard_map/fmn,nc->fmc/dot_general | solution.py:94
  507.4 8.2 %fusion.64 = f32[2,128,256]{2,1,0:T(8,128)S(1)} fusion(s32[256]{0:T(256)S(1)} %iota_add_fusion, bf16[2,2,128,2048]{3,2,0,1:T(8,128)(2,1)S(1)} %all-reduce.3), kind=kOutput, calls=%fused_computation.105 | convolution fusion | flops 276824064 | bytes 1311744 | tf_op jit(solution)/shard_map/fmn,nc->fmc/dot_general | solution.py:94
  515.6 8.4 %fusion.40 = bf16[2,1,128,256]{3,2,0,1:T(8,128)(2,1)S(1)} fusion(f32[2,128,256]{2,1,0:T(8,128)S(1)} %fusion.56, s32[256]{0:T(256)S(1)} %iota_add_fusion, bf16[2,2,128,2048]{3,2,0,1:T(8,128)(2,1)S(1)} %all-reduce.3), kind=kOutput, calls=%fused_computation.76 | convolution fusion | flops 276955136 | bytes 1442816 | tf_op jit(solution)/shard_map/fmn,nc->fmc/dot_general | solution.py:94
  523.9 7.9 %fusion.39 = bf16[2,1,128,256]{3,2,0,1:T(8,128)(2,1)S(1)} fusion(f32[2,128,256]{2,1,0:T(8,128)S(1)} %fusion.64, s32[256]{0:T(256)S(1)} %iota_add_fusion, bf16[2,2,128,2048]{3,2,0,1:T(8,128)(2,1)S(1)} %all-reduce.3), kind=kOutput, calls=%fused_computation.75 | convolution fusion | flops 276955136 | bytes 1442816 | tf_op jit(solution)/shard_map/fmn,nc->fmc/dot_general | solution.py:94
  531.8 0.7 pad_maximum_fusion.4
  532.6 51.3 %all-gather.27.cloned.1.call-done = bf16[2,2,2048,256]{3,2,0,1:T(8,128)(2,1)} async-done(((bf16[2,2,128,256]{3,2,0,1:T(8,128)(2,1)}), bf16[2,2,2048,256]{3,2,0,1:T(8,128)(2,1)}) %all-gather.27.cloned.1.call-update) | async-done | bytes 4194320 | tf_op jit(solution)/shard_map/all_gather | solution.py:170
  583.8 6.2 fusion.16
  590.0 4.3 fusion.15
  594.3 4.3 fusion.20
  598.6 4.5 fusion.22
  603.5 7.6 %all-gather.12 = f32[4,2,2]{2,1,0:T(2,128)S(1)} all-gather(f32[1,2,2]{2,1,0:T(2,128)S(1)} %maximum_bitcast_fusion.5), channel_id=6, replica_groups=mesh['src_0'=4,'src_1'=4,'rcv_0'=4,'rcv_1'=2] {'src_0'}, dimensions={0}, use_global_device_ids=true | all-gather | bytes 80 | tf_op jit(solution)/shard_map/all_gather | solution.py:42
  611.1 5.9 all-gather.13
  617.0 7.8 %all-gather.14 = f32[4,2,2]{2,1,0:T(2,128)S(1)} all-gather(f32[1,2,2]{2,1,0:T(2,128)S(1)} %maximum_bitcast_fusion.7), channel_id=8, replica_groups=mesh['src_0'=4,'src_1'=4,'rcv_0'=4,'rcv_1'=2] {'rcv_0'}, dimensions={0}, use_global_device_ids=true | all-gather | bytes 80 | tf_op jit(solution)/shard_map/all_gather | solution.py:42
  624.9 8.2 %all-gather.15 = f32[2,2,2]{2,1,0:T(2,128)S(1)} all-gather(f32[1,2,2]{2,1,0:T(2,128)S(1)} %maximum_bitcast_fusion.8), channel_id=9, replica_groups=mesh['src_0'=4,'src_1'=4,'rcv_0'=4,'rcv_1'=2] {'rcv_1'}, dimensions={0}, use_global_device_ids=true | all-gather | bytes 48 | tf_op jit(solution)/shard_map/all_gather | solution.py:42
  633.3 1.0 copy.35
  634.3 0.6 pad_maximum_fusion.5
  (54 shorter events, 3.9 us)
Async XLA Ops:
  7.2 58.1 %all-gather.21.cloned.1.call-start = ((), (), s32[]{:S(2)}) async-start(), calls=%async_computation.2 | async-start | bytes 4456448 | tf_op jit(solution)/shard_map/all_gather | solution.py:129
  8.9 207.8 %all-gather.23.cloned.1.call-start = ((), (), s32[]{:S(2)}) async-start(), calls=%async_computation.3 | async-start | bytes 4456448 | tf_op jit(solution)/shard_map/all_gather | solution.py:170
  10.0 2.5 copy-start.2
  65.3 2.8 copy-start
  165.2 152.1 %all-gather.25.cloned.1.call-start = ((), (), s32[]{:S(2)}) async-start(), calls=%async_computation.4 | async-start | bytes 4456448 | tf_op jit(solution)/shard_map/all_gather | solution.py:145
  216.7 6.0 copy-start.3
  266.8 317.0 %all-gather.27.cloned.1.call-start = ((), (), s32[]{:S(2)}) async-start(), calls=%async_computation.5 | async-start | bytes 4456448 | tf_op jit(solution)/shard_map/all_gather | solution.py:170
  317.3 6.1 copy-start.4
  432.2 2.2 copy-start.1
  583.8 6.2 copy-start.5
Sparse Core Ops, SparseCore 0:
  10.7 54.5 all-gather.20
  165.3 51.4 all-gather.22
  266.9 50.2 all-gather.24
  532.7 51.0 all-gather.26
where the time goes:
time: 645 us; the launch traced here: 642 us
  blocking collectives  234 us (36%)
  waiting for transfers between devices  205 us (32%)
  matrix products  166 us (26%)
  between operations  14.4 us (2%)
  other arithmetic  13.8 us (2%)
  local copies, waits for them, and re-layouts  9 us (1%)
    dot_general x28, matrix products, single(): jnp.einsum(pattern, first_op, second_op, preferred_element_type=jnp.float32)  157 us
    psum x2, blocking collectives, per_device(): gradient_rows = lax.psum(embedded - scaled, RCV)  113 us
    all_gather x2, waiting for transfers between devices, per_device(): lax.all_gather(halfway, SRC, axis=2, tiled=True)  103 us
    all_to_all x2, blocking collectives, copy_for_each(): return lax.all_to_all(copies, axis, split_axis=0, concat_axis=0, tiled=True)  61.9 us
    all_gather x8, blocking collectives, all_in_one(): both, at, found = (lax.all_gather(jnp.concatenate(lines), axis), 0, {})  59 us
    all_gather x1, waiting for transfers between devices, per_device(): columns_all = lax.all_gather(traces, SRC, axis=2, tiled=True)  51.9 us
    all_gather x1, waiting for transfers between devices, per_device(): lax.all_gather(coeff_half, SRC, axis=2, tiled=True)  50.2 us
  transfers between devices with their start and end apart: 4, of which 4 were waited for; matrix products, arithmetic and copies ran while one was open for 1% of the time, Pallas kernels for 0%

commit v1 on v0

v1 whole, which is shorter than its diff:
```python
import functools
import math

import jax
import jax.numpy as jnp
import numpy as np
from jax import lax
from jax.experimental import pallas as pl
from jax.experimental.pallas import tpu as pltpu
from jax.sharding import PartitionSpec as P

MESH = pl.DeviceIdType.MESH
N = 2048
BASE = 64
STEP = 0.4
SHRINK = 0.2
BF = jnp.bfloat16
F32 = jnp.float32


def table_parts():
    cols = np.arange(N)
    low = 2.0 * math.pi * ((np.arange(BASE)[:, None] * cols[None, :]) % N) / N
    high = 2.0 * math.pi * ((np.arange(0, N, BASE)[:, None] * cols[None, :]) % N) / N
    scale = 1.0 / math.sqrt(N)
    parts = (np.cos(low) * scale, np.sin(low) * scale, np.cos(high), np.sin(high))
    return [a.astype(np.float32) for a in parts]


def kernel(
    tr, wave, base_c, base_s, mul_c, mul_s, out, norms,
    tf, tab_c, tab_s, pg, sb, ra, rb, qa, qb, dl, dr, gb, yb, zz, zt, xt,
    trial, coef, cfo, cb, hb, wt, hh, mb, mf, ot, st1, st2, sr1, sr2, nt, nr,
    ssem, rsem,
):
    p = lax.axis_index("src")
    rcv = lax.axis_index("rcv")
    y = rcv // 2
    c = rcv % 2
    z = p // 4
    x = p % 4
    used = [0]
    pending = []

    def ids(n):
        used[0] += n
        return used[0] - n

    def dev(pp, yy, cc):
        return (pp, yy * 2 + cc)

    def rcopy(src, dst, s_id, r_id, where):
        return pltpu.make_async_remote_copy(
            src_ref=src, dst_ref=dst, send_sem=ssem.at[s_id], recv_sem=rsem.at[r_id],
            device_id=where, device_id_type=MESH,
        )

    def send(src, dst, s_id, where):
        copy = rcopy(src, dst, s_id, s_id, where)
        copy.start()
        pending.append(copy)

    def arrived(ref, r_id):
        rcopy(ref, ref, r_id, r_id, dev(p, y, 1 - c)).wait_recv()

    def sent():
        for copy in pending:
            copy.wait_send()
        pending.clear()

    def ds(start, size, unit):
        return pl.ds(pl.multiple_of(start, unit), size)

    barrier = pltpu.get_barrier_semaphore()
    me = p * 2 + c

    @pl.loop(1, 32)
    def _(k):
        other = (me + k) % 32
        pl.semaphore_signal(
            barrier, inc=1, device_id=dev(other // 2, y, other % 2), device_id_type=MESH
        )

    for d in (1, 2, 3):
        pl.semaphore_signal(
            barrier, inc=1, device_id=dev(p, (y + d) % 4, c), device_id_type=MESH
        )
    pl.semaphore_wait(barrier, 34)

    own_rows = ds(128 * p, 128, 128)
    swap = []
    for part in range(2):
        s_id = ids(1)
        where = tf.at[own_rows, ds(part * 512 + 256 * c, 256, 256)]
        send(tr.at[1 - c, part], where, s_id, dev(p, y, 1 - c))
        swap.append(s_id)
    for part in range(2):
        tf[own_rows, ds(part * 512 + 256 * c, 256, 256)] = tr[c, part]
    for part in range(2):
        arrived(tf.at[own_rows, ds(part * 512 + 256 * (1 - c), 256, 256)], swap[part])

    def shift(at, axis, d):
        zz_, xx_ = at
        return ((zz_ + d) % 4, xx_) if axis == 0 else (zz_, (xx_ + d) % 4)

    def neighbour(axis, d):
        a, b = shift((z, x), axis, d)
        return dev(a * 4 + b, y, c)

    def block(at, half, quarter=None):
        start = (at[0] * 4 + at[1]) * 128 + 64 * half
        if quarter is None:
            return tf.at[ds(start, 64, 32), :]
        return tf.at[ds(start + 32 * quarter, 32, 32), :]

    def ag_start(at, axis, half):
        s_id = ids(4)
        send(block(at, half), block(at, half), s_id, neighbour(axis, 1))
        send(block(at, half), block(at, half), s_id + 1, neighbour(axis, -1))
        return at, axis, half, s_id

    def ag_forward(item):
        at, axis, half, s_id = item
        left, right = shift(at, axis, -1), shift(at, axis, 1)
        arrived(block(left, half), s_id)
        send(block(left, half, 0), block(left, half, 0), s_id + 2, neighbour(axis, 1))
        arrived(block(right, half), s_id + 1)
        send(block(right, half, 1), block(right, half, 1), s_id + 3, neighbour(axis, -1))

    def ag_finish(item):
        at, axis, half, s_id = item
        far = shift(at, axis, 2)
        arrived(block(far, half, 0), s_id + 2)
        arrived(block(far, half, 1), s_id + 3)

    def make_table(first, last):
        @pl.loop(first, last)
        def _(m):
            for col in range(0, N, 512):
                here = pl.ds(col, 512)
                bc, bs = base_c[:, here], base_s[:, here]
                mc, ms = mul_c[pl.ds(m, 1), here], mul_s[pl.ds(m, 1), here]
                rows = ds(m * BASE, BASE, BASE)
                tab_c[rows, here] = (bc * mc - bs * ms).astype(BF)
                tab_s[rows, here] = (bs * mc + bc * ms).astype(BF)

    home = (z, x)
    first_x = ag_start(home, 1, 0)
    first_z = ag_start(home, 0, 1)
    second = [ag_start(home, 0, 0), ag_start(home, 1, 1)]
    make_table(0, 24)
    ag_forward(first_x)
    ag_forward(first_z)
    for d in (-1, 1):
        second.append(ag_start(shift(home, 1, d), 0, 0))
        second.append(ag_start(shift(home, 0, d), 1, 1))
    make_table(24, 32)
    ag_forward(second[0])
    ag_forward(second[1])
    ag_finish(first_x)
    ag_finish(first_z)
    second.append(ag_start(shift(home, 1, 2), 0, 0))
    second.append(ag_start(shift(home, 0, 2), 1, 1))
    for item in second[2:]:
        ag_forward(item)
    for item in second:
        ag_finish(item)

    root = 1.0 / math.sqrt(N)
    wr = wave[c, 0] * root
    wi = wave[c, 1] * root

    def dot(a, b):
        return lax.dot_general(a, b, (((1,), (0,)), ((), ())), preferred_element_type=F32)

    def dot_nt(a, b):
        return lax.dot_general(a, b, (((1,), (1,)), ((), ())), preferred_element_type=F32)

    def transform(rows_ref, half, sign, col):
        rows = rows_ref[...].reshape(2 * half, N)
        a = dot(rows, tab_c[:, ds(col, 256, 256)])
        b = dot(rows, tab_s[:, ds(col, 256, 256)])
        if sign > 0:
            return a[:half] + b[half:], a[half:] - b[:half]
        return a[:half] - b[half:], a[half:] + b[:half]

    def plane_exchange(source, landing, first_id):
        @pl.loop(1, 16)
        def _(k):
            q = (p + k) % 16
            rcopy(source(q), landing(p), first_id + k, first_id + k, dev(q, y, c)).start()

    def plane_wait(source, landing, first_id):
        @pl.loop(1, 16)
        def _(k):
            q = (p + 16 - k) % 16
            w = rcopy(source((p + k) % 16), landing(q), first_id + k, first_id + k, dev(q, y, c))
            w.wait_recv()
            w.wait_send()

    totals = []
    for it in range(2):
        if it == 0:
            re = tf[own_rows, 0:512]
            im = tf[own_rows, 512:1024]
            mf[0] = re
            mf[1] = im
            ref, imf = re.astype(F32), im.astype(F32)
            squares = jnp.sum(ref * ref + imf * imf)
        else:
            @pl.loop(0, 8)
            def _(n):
                a, b = transform(cb, 32, -1, n * 256)
                hb[0, :, ds(n * 256, 256, 256)] = a.astype(BF)
                hb[1, :, ds(n * 256, 256, 256)] = b.astype(BF)

            wid = ids(16)
            src_of = lambda q: hb.at[:, :, ds(128 * q, 128, 128)]
            dst_of = lambda q: wt.at[:, ds(32 * q, 32, 32), :]
            plane_exchange(src_of, dst_of, wid)
            wt[:, ds(32 * p, 32, 32), :] = hb[:, :, ds(128 * p, 128, 128)]
            plane_wait(src_of, dst_of, wid)
            for part in range(2):
                hh[part, :, ds(512 * y, 512, 512)] = wt[part].astype(F32).T.astype(BF)
            gid = ids(4)

            def col_block(yy, rows=None):
                if rows is None:
                    return hh.at[:, :, ds(512 * yy, 512, 512)]
                return hh.at[:, pl.ds(64 * rows, 64), ds(512 * yy, 512, 512)]

            up, down, far = (y + 1) % 4, (y + 3) % 4, (y + 2) % 4
            send(col_block(y), col_block(y), gid, dev(p, up, c))
            send(col_block(y), col_block(y), gid + 1, dev(p, down, c))
            arrived(col_block(down), gid)
            send(col_block(down, 0), col_block(down, 0), gid + 2, dev(p, up, c))
            arrived(col_block(up), gid + 1)
            send(col_block(up, 1), col_block(up, 1), gid + 3, dev(p, down, c))
            arrived(col_block(far, 0), gid + 2)
            arrived(col_block(far, 1), gid + 3)

            @pl.loop(0, 8)
            def _(n):
                a, b = transform(hh, 128, -1, n * 256)
                mb[0, :, ds(n * 256, 256, 256)] = a.astype(BF)
                mb[1, :, ds(n * 256, 256, 256)] = b.astype(BF)

            squares = 0.0
            for n in range(2):
                rows = mb[...].reshape(256, N)
                a = dot(rows, tf[:, n * 256 : n * 256 + 256])
                b = dot(rows, tf[:, 512 + n * 256 : 768 + n * 256])
                pr, pi = a[:128] - b[128:], b[:128] + a[128:]
                here = ds(512 * y + n * 256, 256, 256)
                mr = tf[own_rows, n * 256 : n * 256 + 256].astype(F32) - mb[0, :, here].astype(F32)
                mi = tf[own_rows, 512 + n * 256 : 768 + n * 256].astype(F32) - mb[1, :, here].astype(F32)
                mr = mr + (wr * pr - wi * pi)
                mi = mi + (wr * pi + wi * pr)
                squares = squares + jnp.sum(mr * mr + mi * mi)
                mf[0, :, n * 256 : n * 256 + 256] = mr.astype(BF)
                mf[1, :, n * 256 : n * 256 + 256] = mi.astype(BF)

        @pl.loop(0, 8)
        def _(n):
            rows = mf[...].reshape(256, 512)
            here = ds(n * 256, 256, 256)
            a = dot_nt(rows, tf[here, 0:512])
            b = dot_nt(rows, tf[here, 512:1024])
            br, bi = a[:128] + b[128:], a[128:] - b[:128]
            pg[0, :, here] = -(wr * br + wi * bi)
            pg[1, :, here] = -(wr * bi - wi * br)

        mine = ds(512 * y, 512, 512)
        pg[:, :, mine] = pg[:, :, mine] + mf[...].astype(F32)

        up, down, far = (y + 1) % 4, (y + 3) % 4, (y + 2) % 4
        lo, hi = pl.ds(0, 1024), pl.ds(1024, 1024)
        rows_of = lambda yy: ds(32 * yy, 32, 32)
        sb[it] = pg[...].astype(BF)
        sbi = sb.at[it]
        rid = ids(6)
        send(sbi.at[:, rows_of(far), lo], ra.at[it], rid, dev(p, up, c))
        send(sbi.at[:, rows_of(far), hi], rb.at[it], rid + 1, dev(p, down, c))
        send(sbi.at[:, rows_of(up), hi], dl.at[it, :, :, hi], rid + 2, dev(p, up, c))
        send(sbi.at[:, rows_of(down), lo], dr.at[it, :, :, lo], rid + 3, dev(p, down, c))
        arrived(ra.at[it], rid)
        qa[it] = (pg[:, rows_of(up), lo] + ra[it].astype(F32)).astype(BF)
        send(qa.at[it], dl.at[it, :, :, lo], rid + 4, dev(p, up, c))
        arrived(rb.at[it], rid + 1)
        qb[it] = (pg[:, rows_of(down), hi] + rb[it].astype(F32)).astype(BF)
        send(qb.at[it], dr.at[it, :, :, hi], rid + 5, dev(p, down, c))
        arrived(dl.at[it, :, :, hi], rid + 2)
        arrived(dr.at[it, :, :, lo], rid + 3)
        arrived(dl.at[it, :, :, lo], rid + 4)
        arrived(dr.at[it, :, :, hi], rid + 5)
        gb[...] = (pg[:, rows_of(y), :] + dl[it].astype(F32) + dr[it].astype(F32)).astype(BF)

        yid = ids(4)
        for d in (2, 1, 3, 0):
            yy = (y + d) % 4

            @pl.loop(0, 2)
            def _(n):
                a, b = transform(gb, 32, 1, yy * 512 + n * 256)
                yb[it, 0, :, ds(yy * 512 + n * 256, 256, 256)] = a.astype(BF)
                yb[it, 1, :, ds(yy * 512 + n * 256, 256, 256)] = b.astype(BF)

            if d:
                send(
                    yb.at[it, :, :, ds(512 * yy, 512, 512)],
                    zz.at[it, :, rows_of(y), :], yid + d, dev(p, yy, c),
                )
            else:
                zz[it, :, rows_of(y), :] = yb[it, :, :, ds(512 * yy, 512, 512)]
        for d in (1, 3, 2):
            arrived(zz.at[it, :, rows_of((y + 4 - d) % 4), :], yid + d)
        for part in range(2):
            zt[it, part] = zz[it, part].astype(F32).T.astype(BF)
        xid = ids(16)
        src_of = lambda q: zt.at[it, :, ds(32 * q, 32, 32), :]
        dst_of = lambda q: xt.at[it, :, :, ds(128 * q, 128, 128)]
        plane_exchange(src_of, dst_of, xid)
        xt[it, :, :, ds(128 * p, 128, 128)] = zt[it, :, ds(32 * p, 32, 32), :]
        plane_wait(src_of, dst_of, xid)

        def column_step(n, peak):
            here = ds(n * 256, 256, 256)
            a, b = transform(xt.at[it], 32, 1, n * 256)
            a, b = STEP * a, STEP * b
            if it:
                a, b = coef[0, :, here] + a, coef[1, :, here] + b
            trial[0, :, here] = a
            trial[1, :, here] = b
            return jnp.maximum(peak, jnp.sqrt(a * a + b * b))

        peak = jnp.max(lax.fori_loop(0, 8, column_step, jnp.zeros((32, 256), F32)))

        st1[it, 0] = jnp.full((8, 128), peak, F32)
        st1[it, 1] = jnp.full((8, 128), squares, F32)
        sid = ids(16)
        src_of = lambda q: st1.at[it]
        dst_of = lambda q: sr1.at[it, q]
        plane_exchange(src_of, dst_of, sid)
        sr1[it, p] = st1[it]
        plane_wait(src_of, dst_of, sid)
        peak_t, sum_t = sr1[it, 0, 0], sr1[it, 0, 1]
        for k in range(1, 16):
            peak_t = jnp.maximum(peak_t, sr1[it, k, 0])
            sum_t = sum_t + sr1[it, k, 1]
        st2[it, 0] = peak_t
        st2[it, 1] = sum_t
        tid = ids(4)
        for d in (1, 2, 3):
            send(st2.at[it], sr2.at[it, y], tid + d, dev(p, (y + d) % 4, c))
        sr2[it, y] = st2[it]
        for d in (1, 2, 3):
            arrived(sr2.at[it, (y + 4 - d) % 4], tid + d)
        peak_t, sum_t = sr2[it, 0, 0], sr2[it, 0, 1]
        for k in range(1, 4):
            peak_t = jnp.maximum(peak_t, sr2[it, k, 0])
            sum_t = sum_t + sr2[it, k, 1]
        totals.append(sum_t)
        level = SHRINK * jnp.max(peak_t)

        @pl.loop(0, 8)
        def _(n):
            here = ds(n * 256, 256, 256)
            a, b = trial[0, :, here], trial[1, :, here]
            size = jnp.sqrt(a * a + b * b)
            factor = jnp.maximum(1.0 - level / jnp.maximum(size, level), 0.0)
            a, b = a * factor, b * factor
            if it == 0:
                coef[0, :, here] = a
                coef[1, :, here] = b
                cb[0, :, here] = a.astype(BF)
                cb[1, :, here] = b.astype(BF)
            else:
                cfo[0, :, here] = a
                cfo[1, :, here] = b

    nid = ids(1)
    for it in range(2):
        nt[it] = jnp.sqrt(totals[it])
    send(nt, nr, nid, dev(p, y, 1 - c))
    oid = ids(16)
    co = p // 8
    lane = (p % 8) * 2 + c

    def out_copy(q):
        return rcopy(
            cfo.at[:, :, ds(128 * q, 128, 128)],
            ot.at[c, :, ds(32 * (p % 8), 32, 32), :],
            oid + (q + 16 - p) % 16, oid + lane, dev(q, y, co),
        )

    away = co != c

    @pl.loop(1, 16)
    def _(k):
        out_copy((p + k) % 16).start()

    @pl.when(away)
    def _():
        out_copy(p).start()

    @pl.when(jnp.logical_not(away))
    def _():
        ot[c, :, ds(32 * (p % 8), 32, 32), :] = cfo[:, :, ds(128 * p, 128, 128)]

    arrived(nr, nid)
    for it in range(2):
        norms[it, c] = jnp.max(nt[it])
        norms[it, 1 - c] = jnp.max(nr[it])

    @pl.loop(0, 16)
    def _(k):
        q, f = 8 * c + k // 2, k % 2

        @pl.when(jnp.logical_or(q != p, f != c))
        def _():
            there = ot.at[f, :, ds(32 * (q % 8), 32, 32), :]
            rcopy(there, there, oid + k, oid + k, dev(p, y, 1 - c)).wait_recv()

    for f in range(2):
        for part in range(2):
            out[f, part] = ot[f, part].T

    @pl.loop(1, 16)
    def _(k):
        out_copy((p + k) % 16).wait_send()

    @pl.when(away)
    def _():
        out_copy(p).wait_send()

    sent()


def scratch():
    v = lambda *shape, t=BF: pltpu.VMEM(shape, t)
    return [
        v(N, 1024), v(N, N), v(N, N), v(2, 128, N, t=F32), v(2, 2, 128, N),
        v(2, 2, 32, 1024), v(2, 2, 32, 1024), v(2, 2, 32, 1024), v(2, 2, 32, 1024),
        v(2, 2, 32, N), v(2, 2, 32, N), v(2, 32, N), v(2, 2, 32, N),
        v(2, 2, 128, 512), v(2, 2, 512, 128), v(2, 2, 32, N),
        v(2, 32, N, t=F32), v(2, 32, N, t=F32), v(2, 32, N, t=F32), v(2, 32, N),
        v(2, 32, N), v(2, 512, 128), v(2, 128, N), v(2, 128, N), v(2, 128, 512),
        v(2, 2, 256, 128, t=F32),
        v(2, 2, 8, 128, t=F32), v(2, 2, 8, 128, t=F32),
        v(2, 16, 2, 8, 128, t=F32), v(2, 4, 2, 8, 128, t=F32),
        v(2, 8, 128, t=F32), v(2, 8, 128, t=F32),
        pltpu.SemaphoreType.DMA((192,)), pltpu.SemaphoreType.DMA((192,)),
    ]


def per_device(traces, wavelet):
    vm = pl.BlockSpec(memory_space=pltpu.VMEM)
    sm = pl.BlockSpec(memory_space=pltpu.SMEM)
    return pl.pallas_call(
        kernel,
        out_shape=(
            jax.ShapeDtypeStruct((2, 2, 128, 256), F32),
            jax.ShapeDtypeStruct((2, 2), F32),
        ),
        in_specs=[vm, sm, vm, vm, vm, vm],
        out_specs=(vm, sm),
        scratch_shapes=scratch(),
        compiler_params=pltpu.CompilerParams(
            collective_id=0, has_side_effects=True, vmem_limit_bytes=60 * 1024 * 1024
        ),
        name="whole",
    )(traces, wavelet, *table_parts())


def solution(mesh):
    return jax.shard_map(
        per_device,
        mesh=mesh,
        in_specs=(P(None, None, "src", "rcv"), P()),
        out_specs=(P(None, None, "src", "rcv"), P()),
        check_vma=False,
    )
```

time: 645 us -> 155 us (0.24)
  blocking collectives: 234 us -> 0 us
  waiting for transfers between devices: 205 us -> 0 us
  matrix products: 166 us -> 0 us
  Pallas kernels: 0 us -> 151 us
  other arithmetic: 13.8 us -> 0 us
  between operations: 14.4 us -> 0.65 us
  local copies, waits for them, and re-layouts: 9 us -> 2.44 us
    all_gather x4 -> x0, waiting for transfers between devices: 205 us -> none  [the longest x2 103 us: per_device(): lax.all_gather(halfway, SRC, axis=2, tiled=True)]
    dot_general x36 -> x0, matrix products: 166 us -> none  [the longest x28 157 us: single(): jnp.einsum(pattern, first_op, second_op, preferred_element_type=jnp.float32)]
    pallas_call x0 -> x1, Pallas kernels: none -> 151 us  [per_device(): pl.pallas_call(kernel, out_shape=(jax.ShapeDtypeStruct((2, 2, 128, 256),...]
    psum x2 -> x0, blocking collectives: 113 us -> none  [per_device(): gradient_rows = lax.psum(embedded - scaled, RCV)]
    all_to_all x2 -> x0, blocking collectives: 61.9 us -> none  [copy_for_each(): return lax.all_to_all(copies, axis, split_axis=0, concat_axis=0, tiled=True)]
    all_gather x8 -> x0, blocking collectives: 59 us -> none  [all_in_one(): both, at, found = (lax.all_gather(jnp.concatenate(lines), axis), 0, {})]
    sub x2 -> x0, other arithmetic: 7.73 us -> none  [per_device(): gradient_rows = lax.psum(embedded - scaled, RCV)]
  transfers between devices with their start and end apart: 4 -> 0, of which waited for: 4 -> 0; matrix products, arithmetic and copies ran while one was open for 1% -> 0% of each run, Pallas kernels for 0% -> 0%
where the time goes in v1:
time: 155 us
  Pallas kernels  151 us (97%)
  local copies, waits for them, and re-layouts  2.44 us (2%)
    pallas_call x1, Pallas kernels, per_device(): pl.pallas_call(kernel, out_shape=(jax.ShapeDtypeStruct((2, 2, 128, 256),...  151 us

profile of v1, /device:TPU:1, one launch (start us, length us, event | category | flops | bytes accessed | tf_op | source)
XLA Modules:
  0.0 154.6 jit_solution(1815660629751148921)
XLA Ops:
  0.6 151.5 %whole.1 = (f32[2,2,128,256]{3,2,1,0:T(8,128)}, f32[2,2]{1,0:T(2,128)}) custom-call(bf16[2,2,128,256]{3,2,1,0:T(8,128)(2,1)} %tr.1, f32[2,2]{1,0:T(2,128)} %wave.1, f32[64,2048]{1,0:T(8,128)} %constant.8.clone.base_c, f32[64,2048]{1,0:T(8,128)} %constant.9.clone.base_s, f32[32,2048]{1,0:T(8,128)} %constant.10.clone.mul_c, f32[32,2048]{1,0:T(8,128)} %constant.11.clone.mul_s), custom_call_target="tpu_custom_call" | custom-call | tf_op jit(solution)/shard_map/whole/pallas_call | solution.py:459
  152.1 0.0 copy-start
  152.1 1.9 %copy.10 = f32[2,2,128,256]{3,2,1,0:T(8,128)} copy(f32[2,2,128,256]{3,2,1,0:T(8,128)} %get-tuple-element.4) | data formatting | bytes 1048576
  154.0 0.0 copy-done
  154.0 0.6 copy.11
Async XLA Ops:
  152.1 1.9 %copy-start = (f32[2,2]{1,0:T(2,128)S(1)}, f32[2,2]{1,0:T(2,128)}, u32[]{:S(2)}) copy-start(f32[2,2]{1,0:T(2,128)} %get-tuple-element.5) | copy-start | bytes 52

commit v2 on v1

--- a/solution.py
+++ b/solution.py
@@ -11,7 +11,8 @@
 
 MESH = pl.DeviceIdType.MESH
 N = 2048
-BASE = 64
+BASE = 32
+QUARTER = N // 4
 STEP = 0.4
 SHRINK = 0.2
 BF = jnp.bfloat16
@@ -19,18 +20,26 @@
 
 
 def table_parts():
-    cols = np.arange(N)
-    low = 2.0 * math.pi * ((np.arange(BASE)[:, None] * cols[None, :]) % N) / N
-    high = 2.0 * math.pi * ((np.arange(0, N, BASE)[:, None] * cols[None, :]) % N) / N
+    def both(left, right, scale):
+        angle = 2.0 * math.pi * ((left[:, None] * right[None, :]) % N) / N
+        return [(f(angle) * scale).astype(np.float32) for f in (np.cos, np.sin)]
+
     scale = 1.0 / math.sqrt(N)
-    parts = (np.cos(low) * scale, np.sin(low) * scale, np.cos(high), np.sin(high))
-    return [a.astype(np.float32) for a in parts]
+    quarter = np.arange(QUARTER)
+    residue = np.arange(4)
+    order = (4 * quarter[None, :] + residue[:, None]).reshape(-1)
+    first = (4 * np.arange(BASE)[None, :] + residue[:, None]).reshape(-1)
+    later = BASE * np.arange(QUARTER // BASE)
+    return [
+        *both(np.arange(BASE), order, scale), *both(later, order, 1.0),
+        *both(first, quarter, scale), *both(4 * later, quarter, 1.0),
+    ]
 
 
 def kernel(
-    tr, wave, base_c, base_s, mul_c, mul_s, out, norms,
-    tf, tab_c, tab_s, pg, sb, ra, rb, qa, qb, dl, dr, gb, yb, zz, zt, xt,
-    trial, coef, cfo, cb, hb, wt, hh, mb, mf, ot, st1, st2, sr1, sr2, nt, nr,
+    tr, wave, base_c, base_s, mul_c, mul_s, ibase_c, ibase_s, imul_c, imul_s, out, norms,
+    tf, tab_c, tab_s, inv_c, inv_s, perm, pg, sb, ra, rb, qa, qb, dl, dr, ub, yb, zz, zt, xt,
+    trial, cfo, cb, hb, wt, hh, mb, mf, ot, nat, keep, got, st1, st2, sr1, sr2, nt, nr,
     ssem, rsem,
 ):
     p = lax.axis_index("src")
@@ -42,6 +51,15 @@
     used = [0]
     pending = []
 
+    stage = [None]
+
+    def mark(name):
+        if stage[0] is not None:
+            stage[0].__exit__(None, None, None)
+        stage[0] = jax.named_scope(name) if name else None
+        if name:
+            stage[0].__enter__()
+
     def ids(n):
         used[0] += n
         return used[0] - n
@@ -71,6 +89,7 @@
     def ds(start, size, unit):
         return pl.ds(pl.multiple_of(start, unit), size)
 
+    mark("entry")
     barrier = pltpu.get_barrier_semaphore()
     me = p * 2 + c
 
@@ -87,6 +106,7 @@
         )
     pl.semaphore_wait(barrier, 34)
 
+    mark("swap")
     own_rows = ds(128 * p, 128, 128)
     swap = []
     for part in range(2):
@@ -136,25 +156,41 @@
     def make_table(first, last):
         @pl.loop(first, last)
         def _(m):
+            rows = ds(m * BASE, BASE, BASE)
             for col in range(0, N, 512):
                 here = pl.ds(col, 512)
                 bc, bs = base_c[:, here], base_s[:, here]
                 mc, ms = mul_c[pl.ds(m, 1), here], mul_s[pl.ds(m, 1), here]
-                rows = ds(m * BASE, BASE, BASE)
                 tab_c[rows, here] = (bc * mc - bs * ms).astype(BF)
                 tab_s[rows, here] = (bs * mc + bc * ms).astype(BF)
-
+            mc, ms = imul_c[pl.ds(m, 1), :], imul_s[pl.ds(m, 1), :]
+            for r in range(4):
+                bc, bs = ibase_c[r * BASE : r * BASE + BASE], ibase_s[r * BASE : r * BASE + BASE]
+                rows = ds(r * QUARTER + m * BASE, BASE, BASE)
+                inv_c[rows, :] = (bc * mc - bs * ms).astype(BF)
+                inv_s[rows, :] = (bs * mc + bc * ms).astype(BF)
+
+    def make_order():
+        row = lax.broadcasted_iota(jnp.int32, (512, 512), 0)
+        col = lax.broadcasted_iota(jnp.int32, (512, 512), 1)
+        perm[...] = jnp.where(col == 4 * (row % 128) + row // 128, 1.0, 0.0).astype(BF)
+
+    mark("gather_a")
     home = (z, x)
     first_x = ag_start(home, 1, 0)
     first_z = ag_start(home, 0, 1)
     second = [ag_start(home, 0, 0), ag_start(home, 1, 1)]
-    make_table(0, 24)
+    make_table(0, 12)
+    mark("gather_b")
     ag_forward(first_x)
     ag_forward(first_z)
     for d in (-1, 1):
         second.append(ag_start(shift(home, 1, d), 0, 0))
         second.append(ag_start(shift(home, 0, d), 1, 1))
-    make_table(24, 32)
+    mark("table_b")
+    make_table(12, 16)
+    make_order()
+    mark("gather_c")
     ag_forward(second[0])
     ag_forward(second[1])
     ag_finish(first_x)
@@ -176,13 +212,41 @@
     def dot_nt(a, b):
         return lax.dot_general(a, b, (((1,), (1,)), ((), ())), preferred_element_type=F32)
 
-    def transform(rows_ref, half, sign, col):
-        rows = rows_ref[...].reshape(2 * half, N)
-        a = dot(rows, tab_c[:, ds(col, 256, 256)])
-        b = dot(rows, tab_s[:, ds(col, 256, 256)])
-        if sign > 0:
-            return a[:half] + b[half:], a[half:] - b[:half]
-        return a[:half] - b[half:], a[half:] + b[:half]
+    def forward(load, store):
+        x = [[load(part, q) for part in range(2)] for q in range(4)]
+        plus = [[x[h][k] + x[h + 2][k] for k in range(2)] for h in range(2)]
+        less = [[x[h][k] - x[h + 2][k] for k in range(2)] for h in range(2)]
+        for k in range(2):
+            ub[0, k] = (plus[0][k] + plus[1][k]).astype(BF)
+            ub[2, k] = (plus[0][k] - plus[1][k]).astype(BF)
+        ub[1, 0] = (less[0][0] + less[1][1]).astype(BF)
+        ub[1, 1] = (less[0][1] - less[1][0]).astype(BF)
+        ub[3, 0] = (less[0][0] - less[1][1]).astype(BF)
+        ub[3, 1] = (less[0][1] + less[1][0]).astype(BF)
+        for r in range(4):
+            rows = ub[r].reshape(64, QUARTER)
+            here = pl.ds(r * QUARTER, QUARTER)
+            a, b = dot(rows, tab_c[:, here]), dot(rows, tab_s[:, here])
+            store(r, a[:32] + b[32:], a[32:] - b[:32])
+
+    def inverse(load, half, store):
+        for col in range(0, QUARTER, 256):
+            e = []
+            for r in range(4):
+                rows = load(r)
+                there = pl.ds(r * QUARTER, QUARTER)
+                a = dot(rows, inv_c[there, col : col + 256])
+                b = dot(rows, inv_s[there, col : col + 256])
+                e.append((a[:half] - b[half:], b[:half] + a[half:]))
+            plus = [[e[h][k] + e[h + 2][k] for k in range(2)] for h in range(2)]
+            less = [[e[h][k] - e[h + 2][k] for k in range(2)] for h in range(2)]
+            store(col, plus[0][0] + plus[1][0], plus[0][1] + plus[1][1])
+            store(QUARTER + col, less[0][0] - less[1][1], less[0][1] + less[1][0])
+            store(2 * QUARTER + col, plus[0][0] - plus[1][0], plus[0][1] - plus[1][1])
+            store(3 * QUARTER + col, less[0][0] + less[1][1], less[0][1] - less[1][0])
+
+    def residue(ref, q):
+        return ref.at[:, q % 4, ds(32 * (q // 4), 32, 32), :]
 
     def plane_exchange(source, landing, first_id):
         @pl.loop(1, 16)
@@ -208,26 +272,30 @@
             ref, imf = re.astype(F32), im.astype(F32)
             squares = jnp.sum(ref * ref + imf * imf)
         else:
-            @pl.loop(0, 8)
-            def _(n):
-                a, b = transform(cb, 32, -1, n * 256)
-                hb[0, :, ds(n * 256, 256, 256)] = a.astype(BF)
-                hb[1, :, ds(n * 256, 256, 256)] = b.astype(BF)
-
+            mark("g_left")
+            def put_half(col, a, b):
+                hb[0, :, col : col + 256] = a.astype(BF)
+                hb[1, :, col : col + 256] = b.astype(BF)
+
+            inverse(lambda r: cb[:, r].reshape(64, QUARTER), 32, put_half)
+
+            mark("g_plane")
             wid = ids(16)
             src_of = lambda q: hb.at[:, :, ds(128 * q, 128, 128)]
-            dst_of = lambda q: wt.at[:, ds(32 * q, 32, 32), :]
+            dst_of = lambda q: residue(wt, q)
             plane_exchange(src_of, dst_of, wid)
-            wt[:, ds(32 * p, 32, 32), :] = hb[:, :, ds(128 * p, 128, 128)]
+            residue(wt, p)[...] = hb[:, :, ds(128 * p, 128, 128)]
             plane_wait(src_of, dst_of, wid)
             for part in range(2):
-                hh[part, :, ds(512 * y, 512, 512)] = wt[part].astype(F32).T.astype(BF)
+                for r in range(4):
+                    hh[part, r, :, ds(128 * y, 128, 128)] = wt[part, r].astype(F32).T.astype(BF)
+            mark("g_gather")
             gid = ids(4)
 
             def col_block(yy, rows=None):
                 if rows is None:
-                    return hh.at[:, :, ds(512 * yy, 512, 512)]
-                return hh.at[:, pl.ds(64 * rows, 64), ds(512 * yy, 512, 512)]
+                    return hh.at[:, :, :, ds(128 * yy, 128, 128)]
+                return hh.at[rows, :, :, ds(128 * yy, 128, 128)]
 
             up, down, far = (y + 1) % 4, (y + 3) % 4, (y + 2) % 4
             send(col_block(y), col_block(y), gid, dev(p, up, c))
@@ -239,12 +307,14 @@
             arrived(col_block(far, 0), gid + 2)
             arrived(col_block(far, 1), gid + 3)
 
-            @pl.loop(0, 8)
-            def _(n):
-                a, b = transform(hh, 128, -1, n * 256)
-                mb[0, :, ds(n * 256, 256, 256)] = a.astype(BF)
-                mb[1, :, ds(n * 256, 256, 256)] = b.astype(BF)
-
+            mark("g_right")
+            def put_model(col, a, b):
+                mb[0, :, col : col + 256] = a.astype(BF)
+                mb[1, :, col : col + 256] = b.astype(BF)
+
+            inverse(lambda r: hh[:, r].reshape(256, QUARTER), 128, put_model)
+
+            mark("misfit")
             squares = 0.0
             for n in range(2):
                 rows = mb[...].reshape(256, N)
@@ -260,6 +330,7 @@
                 mf[0, :, n * 256 : n * 256 + 256] = mr.astype(BF)
                 mf[1, :, n * 256 : n * 256 + 256] = mi.astype(BF)
 
+        mark("back")
         @pl.loop(0, 8)
         def _(n):
             rows = mf[...].reshape(256, 512)
@@ -278,6 +349,7 @@
         rows_of = lambda yy: ds(32 * yy, 32, 32)
         sb[it] = pg[...].astype(BF)
         sbi = sb.at[it]
+        mark("scatter")
         rid = ids(6)
         send(sbi.at[:, rows_of(far), lo], ra.at[it], rid, dev(p, up, c))
         send(sbi.at[:, rows_of(far), hi], rb.at[it], rid + 1, dev(p, down, c))
@@ -293,48 +365,55 @@
         arrived(dr.at[it, :, :, lo], rid + 3)
         arrived(dl.at[it, :, :, lo], rid + 4)
         arrived(dr.at[it, :, :, hi], rid + 5)
-        gb[...] = (pg[:, rows_of(y), :] + dl[it].astype(F32) + dr[it].astype(F32)).astype(BF)
-
+
+        mark("f_right")
         yid = ids(4)
-        for d in (2, 1, 3, 0):
+
+        def gradient(part, q):
+            here = pl.ds(q * QUARTER, QUARTER)
+            theirs = dl[it, part, :, here].astype(F32) + dr[it, part, :, here].astype(F32)
+            return pg[part, rows_of(y), here] + theirs
+
+        def put_transformed(r, a, b):
+            yb[it, 0, r] = a.astype(BF)
+            yb[it, 1, r] = b.astype(BF)
+
+        forward(gradient, put_transformed)
+        mark("f_y")
+        to_y = lambda yy: yb.at[it, :, :, :, ds(128 * yy, 128, 128)]
+        from_y = lambda yy: zz.at[it, :, :, rows_of(yy), :]
+        for d in (2, 1, 3):
             yy = (y + d) % 4
-
-            @pl.loop(0, 2)
-            def _(n):
-                a, b = transform(gb, 32, 1, yy * 512 + n * 256)
-                yb[it, 0, :, ds(yy * 512 + n * 256, 256, 256)] = a.astype(BF)
-                yb[it, 1, :, ds(yy * 512 + n * 256, 256, 256)] = b.astype(BF)
-
-            if d:
-                send(
-                    yb.at[it, :, :, ds(512 * yy, 512, 512)],
-                    zz.at[it, :, rows_of(y), :], yid + d, dev(p, yy, c),
-                )
-            else:
-                zz[it, :, rows_of(y), :] = yb[it, :, :, ds(512 * yy, 512, 512)]
+            send(to_y(yy), from_y(y), yid + d, dev(p, yy, c))
+        from_y(y)[...] = to_y(y)[...]
         for d in (1, 3, 2):
-            arrived(zz.at[it, :, rows_of((y + 4 - d) % 4), :], yid + d)
+            arrived(from_y((y + 4 - d) % 4), yid + d)
         for part in range(2):
-            zt[it, part] = zz[it, part].astype(F32).T.astype(BF)
+            for r in range(4):
+                zt[it, part, r] = zz[it, part, r].astype(F32).T.astype(BF)
+        mark("f_plane")
         xid = ids(16)
-        src_of = lambda q: zt.at[it, :, ds(32 * q, 32, 32), :]
+        src_of = lambda q: residue(zt.at[it], q)
         dst_of = lambda q: xt.at[it, :, :, ds(128 * q, 128, 128)]
         plane_exchange(src_of, dst_of, xid)
-        xt[it, :, :, ds(128 * p, 128, 128)] = zt[it, :, ds(32 * p, 32, 32), :]
+        dst_of(p)[...] = src_of(p)[...]
         plane_wait(src_of, dst_of, xid)
 
-        def column_step(n, peak):
-            here = ds(n * 256, 256, 256)
-            a, b = transform(xt.at[it], 32, 1, n * 256)
+        mark("f_left")
+        peaks = []
+
+        def put_trial(r, a, b):
             a, b = STEP * a, STEP * b
             if it:
-                a, b = coef[0, :, here] + a, coef[1, :, here] + b
-            trial[0, :, here] = a
-            trial[1, :, here] = b
-            return jnp.maximum(peak, jnp.sqrt(a * a + b * b))
-
-        peak = jnp.max(lax.fori_loop(0, 8, column_step, jnp.zeros((32, 256), F32)))
-
+                a, b = trial[0, r] + a, trial[1, r] + b
+            trial[0, r] = a
+            trial[1, r] = b
+            peaks.append(jnp.max(jnp.sqrt(a * a + b * b)))
+
+        forward(lambda part, q: xt[it, part, :, q * QUARTER : q * QUARTER + QUARTER].astype(F32), put_trial)
+        peak = jnp.maximum(jnp.maximum(peaks[0], peaks[1]), jnp.maximum(peaks[2], peaks[3]))
+
+        mark("stats")
         st1[it, 0] = jnp.full((8, 128), peak, F32)
         st1[it, 1] = jnp.full((8, 128), squares, F32)
         sid = ids(16)
@@ -342,6 +421,25 @@
         dst_of = lambda q: sr1.at[it, q]
         plane_exchange(src_of, dst_of, sid)
         sr1[it, p] = st1[it]
+        if it:
+            mark("out_send")
+            oid = ids(16)
+            for b in range(4):
+                x = [trial[part, r, :, 128 * b : 128 * b + 128] for r in range(4) for part in range(2)]
+                x = jnp.concatenate([jnp.concatenate(x[k::2], axis=1) for k in range(2)], axis=0)
+                hi = x.astype(BF)
+                rest = x - hi.astype(F32)
+                mid = rest.astype(BF)
+                low = (rest - mid.astype(F32)).astype(BF)
+                order = perm[...]
+                x = dot(hi, order) + dot(mid, order) + dot(low, order)
+                cfo[0, :, 512 * b : 512 * b + 512] = x[:32]
+                cfo[1, :, 512 * b : 512 * b + 512] = x[32:]
+            out_src = lambda q: cfo.at[:, :, ds(128 * q, 128, 128)]
+            out_dst = lambda q: ot.at[:, q]
+            plane_exchange(out_src, out_dst, oid)
+            out_dst(p)[...] = out_src(p)[...]
+            mark("stats_wait")
         plane_wait(src_of, dst_of, sid)
         peak_t, sum_t = sr1[it, 0, 0], sr1[it, 0, 1]
         for k in range(1, 16):
@@ -360,96 +458,72 @@
             peak_t = jnp.maximum(peak_t, sr2[it, k, 0])
             sum_t = sum_t + sr2[it, k, 1]
         totals.append(sum_t)
+        mark("shrink")
         level = SHRINK * jnp.max(peak_t)
 
-        @pl.loop(0, 8)
-        def _(n):
-            here = ds(n * 256, 256, 256)
-            a, b = trial[0, :, here], trial[1, :, here]
+        def shrunk(a, b):
             size = jnp.sqrt(a * a + b * b)
             factor = jnp.maximum(1.0 - level / jnp.maximum(size, level), 0.0)
-            a, b = a * factor, b * factor
-            if it == 0:
-                coef[0, :, here] = a
-                coef[1, :, here] = b
-                cb[0, :, here] = a.astype(BF)
-                cb[1, :, here] = b.astype(BF)
-            else:
-                cfo[0, :, here] = a
-                cfo[1, :, here] = b
-
+            return a * factor, b * factor
+
+        if it == 0:
+            for r in range(4):
+                a, b = shrunk(trial[0, r], trial[1, r])
+                trial[0, r] = a
+                trial[1, r] = b
+                cb[0, r] = a.astype(BF)
+                cb[1, r] = b.astype(BF)
+
+    mark("out_wait")
     nid = ids(1)
     for it in range(2):
         nt[it] = jnp.sqrt(totals[it])
     send(nt, nr, nid, dev(p, y, 1 - c))
-    oid = ids(16)
-    co = p // 8
-    lane = (p % 8) * 2 + c
-
-    def out_copy(q):
-        return rcopy(
-            cfo.at[:, :, ds(128 * q, 128, 128)],
-            ot.at[c, :, ds(32 * (p % 8), 32, 32), :],
-            oid + (q + 16 - p) % 16, oid + lane, dev(q, y, co),
-        )
-
-    away = co != c
-
-    @pl.loop(1, 16)
-    def _(k):
-        out_copy((p + k) % 16).start()
-
-    @pl.when(away)
-    def _():
-        out_copy(p).start()
-
-    @pl.when(jnp.logical_not(away))
-    def _():
-        ot[c, :, ds(32 * (p % 8), 32, 32), :] = cfo[:, :, ds(128 * p, 128, 128)]
-
+    plane_wait(out_src, out_dst, oid)
+    mark("out_turn")
+    for b in range(4):
+        for r in range(4):
+            a, d = shrunk(ot[0, 4 * b + r], ot[1, 4 * b + r])
+            nat[0, b, pl.ds(r, 32, stride=4), :] = a
+            nat[1, b, pl.ds(r, 32, stride=4), :] = d
+    halves = ids(2)
+
+    def turned(part, half):
+        return jnp.concatenate([nat[part, 2 * half + k].T for k in range(2)], axis=1)
+
+    for part in range(2):
+        keep[part] = turned(part, 1 - c)
+    send(keep, got, halves, dev(p, y, 1 - c))
+    for part in range(2):
+        out[c, part] = turned(part, c)
+    mark("out_swap")
     arrived(nr, nid)
     for it in range(2):
         norms[it, c] = jnp.max(nt[it])
         norms[it, 1 - c] = jnp.max(nr[it])
-
-    @pl.loop(0, 16)
-    def _(k):
-        q, f = 8 * c + k // 2, k % 2
-
-        @pl.when(jnp.logical_or(q != p, f != c))
-        def _():
-            there = ot.at[f, :, ds(32 * (q % 8), 32, 32), :]
-            rcopy(there, there, oid + k, oid + k, dev(p, y, 1 - c)).wait_recv()
-
-    for f in range(2):
-        for part in range(2):
-            out[f, part] = ot[f, part].T
-
-    @pl.loop(1, 16)
-    def _(k):
-        out_copy((p + k) % 16).wait_send()
-
-    @pl.when(away)
-    def _():
-        out_copy(p).wait_send()
-
+    arrived(got, halves)
+    out[1 - c] = got[...]
     sent()
+    mark(None)
 
 
 def scratch():
     v = lambda *shape, t=BF: pltpu.VMEM(shape, t)
+    pair = pltpu.SemaphoreType.DMA((192,))
     return [
-        v(N, 1024), v(N, N), v(N, N), v(2, 128, N, t=F32), v(2, 2, 128, N),
+        v(N, 1024), v(QUARTER, N), v(QUARTER, N), v(N, QUARTER), v(N, QUARTER), v(512, 512),
+        v(2, 128, N, t=F32), v(2, 2, 128, N),
         v(2, 2, 32, 1024), v(2, 2, 32, 1024), v(2, 2, 32, 1024), v(2, 2, 32, 1024),
-        v(2, 2, 32, N), v(2, 2, 32, N), v(2, 32, N), v(2, 2, 32, N),
-        v(2, 2, 128, 512), v(2, 2, 512, 128), v(2, 2, 32, N),
-        v(2, 32, N, t=F32), v(2, 32, N, t=F32), v(2, 32, N, t=F32), v(2, 32, N),
-        v(2, 32, N), v(2, 512, 128), v(2, 128, N), v(2, 128, N), v(2, 128, 512),
-        v(2, 2, 256, 128, t=F32),
+        v(2, 2, 32, N), v(2, 2, 32, N), v(4, 2, 32, QUARTER), v(2, 2, 4, 32, QUARTER),
+        v(2, 2, 4, 128, 128), v(2, 2, 4, 128, 128), v(2, 2, 32, N),
+        v(2, 4, 32, QUARTER, t=F32), v(2, 32, N, t=F32), v(2, 4, 32, QUARTER),
+        v(2, 32, N), v(2, 4, 128, 128), v(2, 4, 128, QUARTER), v(2, 128, N), v(2, 128, 512),
+        v(2, 16, 32, 128, t=F32), v(2, 4, 128, 128, t=F32),
+        v(2, 128, 256, t=F32), v(2, 128, 256, t=F32),
         v(2, 2, 8, 128, t=F32), v(2, 2, 8, 128, t=F32),
         v(2, 16, 2, 8, 128, t=F32), v(2, 4, 2, 8, 128, t=F32),
         v(2, 8, 128, t=F32), v(2, 8, 128, t=F32),
-        pltpu.SemaphoreType.DMA((192,)), pltpu.SemaphoreType.DMA((192,)),
+        pair, pair,
     ]
 
 
@@ -462,7 +536,7 @@
             jax.ShapeDtypeStruct((2, 2, 128, 256), F32),
             jax.ShapeDtypeStruct((2, 2), F32),
         ),
-        in_specs=[vm, sm, vm, vm, vm, vm],
+        in_specs=[vm, sm] + [vm] * 8,
         out_specs=(vm, sm),
         scratch_shapes=scratch(),
         compiler_params=pltpu.CompilerParams(

time: 155 us -> 133 us (0.86)
  Pallas kernels: 151 us -> 130 us
    pallas_call x1, Pallas kernels: 151 us -> 130 us  [per_device(): pl.pallas_call(kernel, out_shape=(jax.ShapeDtypeStruct((2, 2, 128, 256),...]
where the time goes in v2:
time: 133 us
  Pallas kernels  130 us (98%)
  local copies, waits for them, and re-layouts  2.44 us (2%)
    pallas_call x1, Pallas kernels, per_device(): pl.pallas_call(kernel, out_shape=(jax.ShapeDtypeStruct((2, 2, 128, 256),...  130 us

profile of v2, /device:TPU:1, one launch (start us, length us, event | category | flops | bytes accessed | tf_op | source)
XLA Modules:
  0.0 133.3 jit_solution(2502876858499765568)
XLA Ops:
  0.6 130.2 %whole.1 = (f32[2,2,128,256]{3,2,1,0:T(8,128)}, f32[2,2]{1,0:T(2,128)}) custom-call(bf16[2,2,128,256]{3,2,1,0:T(8,128)(2,1)} %tr.1, f32[2,2]{1,0:T(2,128)} %wave.1, f32[32,2048]{1,0:T(8,128)} %constant.16.clone.base_c, f32[32,2048]{1,0:T(8,128)} %constant.17.clone.base_s, f32[16,2048]{1,0:T(8,128)} %constant.18.clone.mul_c, ...), custom_call_target="tpu_custom_call" | custom-call | tf_op jit(solution)/shard_map/whole/pallas_call | solution.py:533
  130.8 0.0 copy-start
  130.8 1.9 %copy.14 = f32[2,2,128,256]{3,2,1,0:T(8,128)} copy(f32[2,2,128,256]{3,2,1,0:T(8,128)} %get-tuple-element.4) | data formatting | bytes 1048576
  132.7 0.0 copy-done
  132.7 0.6 copy.15
Async XLA Ops:
  130.8 1.9 %copy-start = (f32[2,2]{1,0:T(2,128)S(1)}, f32[2,2]{1,0:T(2,128)}, u32[]{:S(2)}) copy-start(f32[2,2]{1,0:T(2,128)} %get-tuple-element.5) | copy-start | bytes 52

commit v3 on v2

v3 whole, which is shorter than its diff:
```python
import functools
import math

import jax
import jax.numpy as jnp
import numpy as np
from jax import lax
from jax.experimental import pallas as pl
from jax.experimental.pallas import tpu as pltpu
from jax.sharding import PartitionSpec as P

MESH = pl.DeviceIdType.MESH
N = 2048
BASE = 32
QUARTER = N // 4
STEP = 0.4
SHRINK = 0.2
BF = jnp.bfloat16
F32 = jnp.float32


def table_parts():
    def both(left, right, scale):
        angle = 2.0 * math.pi * ((left[:, None] * right[None, :]) % N) / N
        return [(f(angle) * scale).astype(np.float32) for f in (np.cos, np.sin)]

    scale = 1.0 / math.sqrt(N)
    quarter = np.arange(QUARTER)
    residue = np.arange(4)
    order = (4 * quarter[None, :] + residue[:, None]).reshape(-1)
    first = (4 * np.arange(BASE)[None, :] + residue[:, None]).reshape(-1)
    later = BASE * np.arange(QUARTER // BASE)
    return [
        *both(np.arange(BASE), order, scale), *both(later, order, 1.0),
        *both(first, quarter, scale), *both(4 * later, quarter, 1.0),
    ]


def kernel(
    tr, wave, base_c, base_s, mul_c, mul_s, ibase_c, ibase_s, imul_c, imul_s, out, norms,
    tf, tab_c, tab_s, inv_c, inv_s, perm, pg, ubt, tp, sb, ra, rb, qa, qb, dl, dr, ub, zt, xt,
    trial, cfo, cb, hb, wt, hh, mb, mf, ot, nat, keep, got, st1, st2, sr1, sr2, nt, nr,
    ssem, rsem,
):
    src = lax.axis_index("src")
    rcv = lax.axis_index("rcv")
    y = rcv // 2
    c = rcv % 2
    z = src // 4
    x = src % 4
    lane2 = (1 - c) * x + c * y
    g = (1 - c) * y + c * x
    p = z * 4 + lane2
    used = [0]
    pending = []

    stage = [None]

    def mark(name):
        if stage[0] is not None:
            stage[0].__exit__(None, None, None)
        stage[0] = jax.named_scope(name) if name else None
        if name:
            stage[0].__enter__()

    def ids(n):
        used[0] += n
        return used[0] - n

    def chip(zz_, xx_, yy_, cc_):
        return (zz_ * 4 + xx_, yy_ * 2 + cc_)

    def dev(q, gg):
        second = q % 4
        return chip(q // 4, (1 - c) * second + c * gg, (1 - c) * gg + c * second, c)

    partner = chip(z, x, y, 1 - c)

    def rcopy(src, dst, s_id, r_id, where):
        return pltpu.make_async_remote_copy(
            src_ref=src, dst_ref=dst, send_sem=ssem.at[s_id], recv_sem=rsem.at[r_id],
            device_id=where, device_id_type=MESH,
        )

    def send(src, dst, s_id, where):
        copy = rcopy(src, dst, s_id, s_id, where)
        copy.start()
        pending.append(copy)

    def arrived(ref, r_id):
        rcopy(ref, ref, r_id, r_id, partner).wait_recv()

    def sent():
        for copy in pending:
            copy.wait_send()
        pending.clear()

    def ds(start, size, unit):
        return pl.ds(pl.multiple_of(start, unit), size)

    mark("entry")
    barrier = pltpu.get_barrier_semaphore()

    def greet(where):
        pl.semaphore_signal(barrier, inc=1, device_id=where, device_id_type=MESH)

    greet(partner)
    for d in (1, 2, 3):
        greet(dev(p, (g + d) % 4))
    for d in (1, 3):
        greet(dev((z + d) % 4 * 4 + lane2, g))
        greet(dev(z * 4 + (lane2 + d) % 4, g))
    crossed = jnp.logical_and(c == 1, x != y)

    @pl.when(crossed)
    def _():
        greet(chip(z, y, x, 0))
        greet(chip(z, y, x, 1))

    @pl.when(x != y)
    def _():
        pl.semaphore_wait(barrier, 9)

    @pl.when(x == y)
    def _():
        pl.semaphore_wait(barrier, 8)

    mark("swap")
    own_rows = ds(128 * p, 128, 128)
    swap = ids(2)
    landing = tf.at[:, ds(128 * src, 128, 128), ds(256 * c, 256, 256)]
    to_first = rcopy(tr.at[0], landing, swap, swap + c, chip(z, x, y, 0))
    to_second = rcopy(tr.at[1], landing, swap + 1, swap + c, chip(z, y, x, 1))
    stays = jnp.logical_and(c == 1, x == y)

    @pl.when(jnp.logical_not(stays))
    def _():
        to_second.start()

    @pl.when(c == 1)
    def _():
        to_first.start()

    @pl.when(c == 0)
    def _():
        landing[...] = tr[0]

    @pl.when(stays)
    def _():
        landing[...] = tr[1]

    @pl.when(c == 1)
    def _():
        arrived(tf.at[:, own_rows, 0:256], swap)

    @pl.when(jnp.logical_not(stays))
    def _():
        arrived(tf.at[:, own_rows, 256:512], swap + 1)

    def shift(at, axis, d):
        zz_, xx_ = at
        return ((zz_ + d + 4) % 4, xx_) if axis == 0 else (zz_, (xx_ + d + 4) % 4)

    def neighbour(axis, d):
        a, b = shift((z, lane2), axis, d)
        return dev(a * 4 + b, g)

    def block(at, kind, part=None):
        start = (at[0] * 4 + at[1]) * 128 + 96 * kind
        rows = 32 if kind else 96
        if part is not None:
            rows = rows // 2
            start = start + rows * part
        return tf.at[:, ds(start, rows, 16), :]

    def ag_start(at, axis, half):
        s_id = ids(4)
        send(block(at, half), block(at, half), s_id, neighbour(axis, 1))
        send(block(at, half), block(at, half), s_id + 1, neighbour(axis, -1))
        return at, axis, half, s_id

    def ag_forward(item):
        at, axis, half, s_id = item
        left, right = shift(at, axis, -1), shift(at, axis, 1)
        arrived(block(left, half), s_id)
        send(block(left, half, 0), block(left, half, 0), s_id + 2, neighbour(axis, 1))
        arrived(block(right, half), s_id + 1)
        send(block(right, half, 1), block(right, half, 1), s_id + 3, neighbour(axis, -1))

    def ag_finish(item):
        at, axis, half, s_id = item
        far = shift(at, axis, 2)
        arrived(block(far, half, 0), s_id + 2)
        arrived(block(far, half, 1), s_id + 3)

    def make_table(first, last):
        @pl.loop(first, last)
        def _(m):
            rows = ds(m * BASE, BASE, BASE)
            for col in range(0, N, 512):
                here = pl.ds(col, 512)
                bc, bs = base_c[:, here], base_s[:, here]
                mc, ms = mul_c[pl.ds(m, 1), here], mul_s[pl.ds(m, 1), here]
                tab_c[rows, here] = (bc * mc - bs * ms).astype(BF)
                tab_s[rows, here] = (bs * mc + bc * ms).astype(BF)
            mc, ms = imul_c[pl.ds(m, 1), :], imul_s[pl.ds(m, 1), :]
            for r in range(4):
                bc, bs = ibase_c[r * BASE : r * BASE + BASE], ibase_s[r * BASE : r * BASE + BASE]
                rows = ds(r * QUARTER + m * BASE, BASE, BASE)
                inv_c[rows, :] = (bc * mc - bs * ms).astype(BF)
                inv_s[rows, :] = (bs * mc + bc * ms).astype(BF)

    def make_order():
        row = lax.broadcasted_iota(jnp.int32, (512, 512), 0)
        col = lax.broadcasted_iota(jnp.int32, (512, 512), 1)
        perm[...] = jnp.where(col == 4 * (row % 128) + row // 128, 1.0, 0.0).astype(BF)

    mark("gather_a")
    home = (z, lane2)
    first = [ag_start(home, 0, 0), ag_start(home, 1, 1)]
    second = [ag_start(home, 1, 0), ag_start(home, 0, 1)]
    make_table(0, 12)
    mark("gather_b")
    for item in first:
        ag_forward(item)
    for d in (-1, 1):
        second.append(ag_start(shift(home, 0, d), 1, 0))
        second.append(ag_start(shift(home, 1, d), 0, 1))
    mark("table_b")
    make_table(12, 16)
    make_order()
    mark("gather_c")
    for item in second[:2]:
        ag_forward(item)
    for item in first:
        ag_finish(item)
    second.append(ag_start(shift(home, 0, 2), 1, 0))
    second.append(ag_start(shift(home, 1, 2), 0, 1))
    for item in second[2:]:
        ag_forward(item)
    for item in second:
        ag_finish(item)

    root = 1.0 / math.sqrt(N)
    wr = wave[c, 0] * root
    wi = wave[c, 1] * root

    def dot(a, b):
        return lax.dot_general(a, b, (((1,), (0,)), ((), ())), preferred_element_type=F32)

    def dot_nt(a, b):
        return lax.dot_general(a, b, (((1,), (1,)), ((), ())), preferred_element_type=F32)

    def quarters(load, ub):
        x = [[load(part, q) for part in range(2)] for q in range(4)]
        plus = [[x[h][k] + x[h + 2][k] for k in range(2)] for h in range(2)]
        less = [[x[h][k] - x[h + 2][k] for k in range(2)] for h in range(2)]
        for k in range(2):
            ub(0, k)[...] = (plus[0][k] + plus[1][k]).astype(BF)
            ub(2, k)[...] = (plus[0][k] - plus[1][k]).astype(BF)
        ub(1, 0)[...] = (less[0][0] + less[1][1]).astype(BF)
        ub(1, 1)[...] = (less[0][1] - less[1][0]).astype(BF)
        ub(3, 0)[...] = (less[0][0] - less[1][1]).astype(BF)
        ub(3, 1)[...] = (less[0][1] + less[1][0]).astype(BF)

    def forward(load, store):
        quarters(load, lambda r, part: ub.at[r, part])
        for r in range(4):
            rows = ub[r].reshape(64, QUARTER)
            here = pl.ds(r * QUARTER, QUARTER)
            a, b = dot(rows, tab_c[:, here]), dot(rows, tab_s[:, here])
            store(r, a[:32] + b[32:], a[32:] - b[:32])

    def inverse(load, half, store):
        for col in range(0, QUARTER, 256):
            e = []
            for r in range(4):
                rows = load(r)
                there = pl.ds(r * QUARTER, QUARTER)
                a = dot(rows, inv_c[there, col : col + 256])
                b = dot(rows, inv_s[there, col : col + 256])
                e.append((a[:half] - b[half:], b[:half] + a[half:]))
            plus = [[e[h][k] + e[h + 2][k] for k in range(2)] for h in range(2)]
            less = [[e[h][k] - e[h + 2][k] for k in range(2)] for h in range(2)]
            store(col, plus[0][0] + plus[1][0], plus[0][1] + plus[1][1])
            store(QUARTER + col, less[0][0] - less[1][1], less[0][1] + less[1][0])
            store(2 * QUARTER + col, plus[0][0] - plus[1][0], plus[0][1] - plus[1][1])
            store(3 * QUARTER + col, less[0][0] + less[1][1], less[0][1] - less[1][0])

    def residue(ref, q):
        return ref.at[:, q % 4, ds(32 * (q // 4), 32, 32), :]

    def plane_exchange(source, landing, first_id):
        @pl.loop(1, 16)
        def _(k):
            q = (p + k) % 16
            rcopy(source(q), landing(p), first_id + k, first_id + k, dev(q, g)).start()

    def plane_wait(source, landing, first_id):
        @pl.loop(1, 16)
        def _(k):
            q = (p + 16 - k) % 16
            w = rcopy(source((p + k) % 16), landing(q), first_id + k, first_id + k, dev(q, g))
            w.wait_recv()
            w.wait_send()

    totals = []
    for it in range(2):
        if it == 0:
            re = tf[0, own_rows, :]
            im = tf[1, own_rows, :]
            mf[0] = re
            mf[1] = im
            ref, imf = re.astype(F32), im.astype(F32)
            squares = jnp.sum(ref * ref + imf * imf)
        else:
            mark("g_left")
            def put_half(col, a, b):
                hb[0, :, col : col + 256] = a.astype(BF)
                hb[1, :, col : col + 256] = b.astype(BF)

            inverse(lambda r: cb[:, r].reshape(64, QUARTER), 32, put_half)

            mark("g_plane")
            wid = ids(16)
            src_of = lambda q: hb.at[:, :, ds(128 * q, 128, 128)]
            dst_of = lambda q: residue(wt, q)
            plane_exchange(src_of, dst_of, wid)
            residue(wt, p)[...] = hb[:, :, ds(128 * p, 128, 128)]
            plane_wait(src_of, dst_of, wid)
            for part in range(2):
                for r in range(4):
                    hh[part, r, :, ds(128 * g, 128, 128)] = wt[part, r].astype(F32).T.astype(BF)
            mark("g_gather")
            gid = ids(4)

            def col_block(yy, rows=None):
                if rows is None:
                    return hh.at[:, :, :, ds(128 * yy, 128, 128)]
                return hh.at[rows, :, :, ds(128 * yy, 128, 128)]

            up, down, far = (g + 1) % 4, (g + 3) % 4, (g + 2) % 4
            send(col_block(g), col_block(g), gid, dev(p, up))
            send(col_block(g), col_block(g), gid + 1, dev(p, down))
            arrived(col_block(down), gid)
            send(col_block(down, 0), col_block(down, 0), gid + 2, dev(p, up))
            arrived(col_block(up), gid + 1)
            send(col_block(up, 1), col_block(up, 1), gid + 3, dev(p, down))
            arrived(col_block(far, 0), gid + 2)
            arrived(col_block(far, 1), gid + 3)

            mark("g_right")
            def put_model(col, a, b):
                mb[0, :, col : col + 256] = a.astype(BF)
                mb[1, :, col : col + 256] = b.astype(BF)

            inverse(lambda r: hh[:, r].reshape(256, QUARTER), 128, put_model)

            mark("misfit")
            squares = 0.0
            for n in range(2):
                rows = mb[...].reshape(256, N)
                some = pl.ds(n * 256, 256)
                a, b = dot(rows, tf[0, :, some]), dot(rows, tf[1, :, some])
                pr, pi = a[:128] - b[128:], b[:128] + a[128:]
                here = ds(512 * g + n * 256, 256, 256)
                mr = tf[0, own_rows, some].astype(F32) - mb[0, :, here].astype(F32)
                mi = tf[1, own_rows, some].astype(F32) - mb[1, :, here].astype(F32)
                mr = mr + (wr * pr - wi * pi)
                mi = mi + (wr * pi + wi * pr)
                squares = squares + jnp.sum(mr * mr + mi * mi)
                mf[0, :, n * 256 : n * 256 + 256] = mr.astype(BF)
                mf[1, :, n * 256 : n * 256 + 256] = mi.astype(BF)

        mark("back")
        @pl.loop(0, 4)
        def _(n):
            errors = mf[...].reshape(256, 512)
            here = ds(n * 512, 512, 512)
            a, b = dot_nt(tf[0, here, :], errors), dot_nt(tf[1, here, :], errors)
            br, bi = a[:, :128] + b[:, 128:], a[:, 128:] - b[:, :128]
            pg[0, here, :] = -(wr * br + wi * bi)
            pg[1, here, :] = -(wr * bi - wi * br)

        mine = ds(512 * g, 512, 512)
        for part in range(2):
            pg[part, mine, :] = pg[part, mine, :] + mf[part].astype(F32).T

        mark("f_right")
        quarters(
            lambda part, q: pg[part, q * QUARTER : q * QUARTER + QUARTER, :],
            lambda r, part: ubt.at[r, :, pl.ds(128 * part, 128)],
        )
        for r in range(4):
            there = pl.ds(r * QUARTER, QUARTER)
            a, b = dot(inv_c[there, :], ubt[r]), dot(inv_s[there, :], ubt[r])
            tr_, ti_ = a[:, :128] + b[:, 128:], a[:, 128:] - b[:, :128]
            tp[0, r] = tr_
            tp[1, r] = ti_
            sb[it, 0, r] = tr_.astype(BF)
            sb[it, 1, r] = ti_.astype(BF)

        mark("scatter")
        up, down, far = (g + 1) % 4, (g + 3) % 4, (g + 2) % 4
        cols_of = lambda gg: ds(128 * gg, 128, 128)
        rid = ids(6)
        send(sb.at[it, 0, :, cols_of(far), :], ra.at[it], rid, dev(p, up))
        send(sb.at[it, 1, :, cols_of(far), :], rb.at[it], rid + 1, dev(p, down))
        send(sb.at[it, 1, :, cols_of(up), :], dl.at[it, 1], rid + 2, dev(p, up))
        send(sb.at[it, 0, :, cols_of(down), :], dr.at[it, 0], rid + 3, dev(p, down))
        arrived(ra.at[it], rid)
        qa[it] = (tp[0, :, cols_of(up), :] + ra[it].astype(F32)).astype(BF)
        send(qa.at[it], dl.at[it, 0], rid + 4, dev(p, up))
        arrived(rb.at[it], rid + 1)
        qb[it] = (tp[1, :, cols_of(down), :] + rb[it].astype(F32)).astype(BF)
        send(qb.at[it], dr.at[it, 1], rid + 5, dev(p, down))
        arrived(dl.at[it, 1], rid + 2)
        arrived(dr.at[it, 0], rid + 3)
        arrived(dl.at[it, 0], rid + 4)
        arrived(dr.at[it, 1], rid + 5)
        zt[it] = (tp[:, :, cols_of(g), :] + dl[it].astype(F32) + dr[it].astype(F32)).astype(BF)
        mark("f_plane")
        xid = ids(16)
        src_of = lambda q: residue(zt.at[it], q)
        dst_of = lambda q: xt.at[it, :, :, ds(128 * q, 128, 128)]
        plane_exchange(src_of, dst_of, xid)
        dst_of(p)[...] = src_of(p)[...]
        plane_wait(src_of, dst_of, xid)

        mark("f_left")
        peaks = []

        def put_trial(r, a, b):
            a, b = STEP * a, STEP * b
            if it:
                a, b = trial[0, r] + a, trial[1, r] + b
            trial[0, r] = a
            trial[1, r] = b
            peaks.append(jnp.max(jnp.sqrt(a * a + b * b)))

        forward(lambda part, q: xt[it, part, :, q * QUARTER : q * QUARTER + QUARTER].astype(F32), put_trial)
        peak = jnp.maximum(jnp.maximum(peaks[0], peaks[1]), jnp.maximum(peaks[2], peaks[3]))

        mark("stats")
        lane = lax.broadcasted_iota(jnp.int32, (1, 128), 1)
        st1[it] = jnp.where(lane < 64, peak, squares)
        sid = ids(16)
        src_of = lambda q: st1.at[it]
        dst_of = lambda q: sr1.at[it, q]
        plane_exchange(src_of, dst_of, sid)
        sr1[it, p] = st1[it]
        if it:
            mark("out_send")
            oid = ids(16)
            for b in range(4):
                v = [trial[part, r, :, 128 * b : 128 * b + 128] for r in range(4) for part in range(2)]
                v = jnp.concatenate([jnp.concatenate(v[k::2], axis=1) for k in range(2)], axis=0)
                hi = v.astype(BF)
                rest = v - hi.astype(F32)
                mid = rest.astype(BF)
                low = (rest - mid.astype(F32)).astype(BF)
                order = perm[...]
                v = dot(hi, order) + dot(mid, order) + dot(low, order)
                cfo[0, :, 512 * b : 512 * b + 512] = v[:32]
                cfo[1, :, 512 * b : 512 * b + 512] = v[32:]
            out_src = lambda q: cfo.at[:, :, ds(128 * q, 128, 128)]
            out_dst = lambda q: ot.at[:, q]
            away = jnp.logical_and(c == 1, x != y)

            def out_copy(q):
                s_id = oid + (q + 16 - p) % 16
                return rcopy(out_src(q), out_dst(p), s_id, oid + p, chip(q // 4, q % 4, g, c))

            @pl.loop(1, 16)
            def _(k):
                out_copy((p + k) % 16).start()

            @pl.when(away)
            def _():
                out_copy(p).start()

            @pl.when(jnp.logical_not(away))
            def _():
                out_dst(p)[...] = out_src(p)[...]

            mark("stats_wait")
        plane_wait(src_of, dst_of, sid)
        def joined(all_of):
            return jnp.where(lane < 64, jnp.max(all_of, axis=0), jnp.sum(all_of, axis=0))

        st2[it] = joined(sr1[it])
        tid = ids(4)
        for d in (1, 2, 3):
            send(st2.at[it], sr2.at[it, g], tid + d, dev(p, (g + d) % 4))
        sr2[it, g] = st2[it]
        for d in (1, 2, 3):
            arrived(sr2.at[it, (g + 4 - d) % 4], tid + d)
        both = joined(sr2[it])
        totals.append(jnp.max(jnp.where(lane < 64, 0.0, both)))
        mark("shrink")
        level = SHRINK * jnp.max(jnp.where(lane < 64, both, 0.0))

        def shrunk(a, b):
            size = jnp.sqrt(a * a + b * b)
            factor = jnp.maximum(1.0 - level / jnp.maximum(size, level), 0.0)
            return a * factor, b * factor

        if it == 0:
            for r in range(4):
                a, b = shrunk(trial[0, r], trial[1, r])
                trial[0, r] = a
                trial[1, r] = b
                cb[0, r] = a.astype(BF)
                cb[1, r] = b.astype(BF)

    mark("out_wait")
    nid = ids(1)
    for it in range(2):
        nt[it] = jnp.sqrt(jnp.full((1, 128), totals[it], F32))
    send(nt, nr, nid, partner)

    @pl.loop(1, 16)
    def _(k):
        q = (p + k) % 16
        arrived(out_dst(q), oid + q)
        out_copy(q).wait_send()

    @pl.when(away)
    def _():
        arrived(out_dst(p), oid + p)
        out_copy(p).wait_send()

    mark("out_turn")
    for b in range(4):
        for r in range(4):
            a, d = shrunk(ot[0, 4 * b + r], ot[1, 4 * b + r])
            nat[0, b, pl.ds(r, 32, stride=4), :] = a
            nat[1, b, pl.ds(r, 32, stride=4), :] = d
    halves = ids(2)

    def turned(part, half):
        return jnp.concatenate([nat[part, 2 * half + k].T for k in range(2)], axis=1)

    for part in range(2):
        keep[part] = turned(part, 1 - c)
    send(keep, got, halves, partner)
    for part in range(2):
        out[c, part] = turned(part, c)
    mark("out_swap")
    arrived(nr, nid)
    for it in range(2):
        norms[it, c] = jnp.max(nt[it])
        norms[it, 1 - c] = jnp.max(nr[it])
    arrived(got, halves)
    out[1 - c] = got[...]
    sent()

    @pl.when(jnp.logical_not(stays))
    def _():
        to_second.wait_send()

    @pl.when(c == 1)
    def _():
        to_first.wait_send()

    mark(None)


def scratch():
    v = lambda *shape, t=BF: pltpu.VMEM(shape, t)
    pair = pltpu.SemaphoreType.DMA((192,))
    return [
        v(2, N, 512), v(QUARTER, N), v(QUARTER, N), v(N, QUARTER), v(N, QUARTER), v(512, 512),
        v(2, N, 128, t=F32), v(4, QUARTER, 256), v(2, 4, QUARTER, 128, t=F32),
        v(2, 2, 4, QUARTER, 128), v(2, 4, 128, 128), v(2, 4, 128, 128), v(2, 4, 128, 128),
        v(2, 4, 128, 128), v(2, 2, 4, 128, 128), v(2, 2, 4, 128, 128), v(4, 2, 32, QUARTER),
        v(2, 2, 4, 128, 128), v(2, 2, 32, N),
        v(2, 4, 32, QUARTER, t=F32), v(2, 32, N, t=F32), v(2, 4, 32, QUARTER),
        v(2, 32, N), v(2, 4, 128, 128), v(2, 4, 128, QUARTER), v(2, 128, N), v(2, 128, 512),
        v(2, 16, 32, 128, t=F32), v(2, 4, 128, 128, t=F32),
        v(2, 128, 256, t=F32), v(2, 128, 256, t=F32),
        v(2, 1, 128, t=F32), v(2, 1, 128, t=F32), v(2, 16, 1, 128, t=F32), v(2, 4, 1, 128, t=F32),
        v(2, 1, 128, t=F32), v(2, 1, 128, t=F32),
        pair, pair,
    ]


def per_device(traces, wavelet):
    vm = pl.BlockSpec(memory_space=pltpu.VMEM)
    sm = pl.BlockSpec(memory_space=pltpu.SMEM)
    return pl.pallas_call(
        kernel,
        out_shape=(
            jax.ShapeDtypeStruct((2, 2, 128, 256), F32),
            jax.ShapeDtypeStruct((2, 2), F32),
        ),
        in_specs=[vm, sm] + [vm] * 8,
        out_specs=(vm, sm),
        scratch_shapes=scratch(),
        compiler_params=pltpu.CompilerParams(
            collective_id=0, has_side_effects=True, vmem_limit_bytes=60 * 1024 * 1024
        ),
        name="whole",
    )(traces, wavelet, *table_parts())


def solution(mesh):
    return jax.shard_map(
        per_device,
        mesh=mesh,
        in_specs=(P(None, None, "src", "rcv"), P()),
        out_specs=(P(None, None, "src", "rcv"), P()),
        check_vma=False,
    )
```

time: 133 us -> 118 us (0.89)
  Pallas kernels: 130 us -> 115 us
    pallas_call x1, Pallas kernels: 130 us -> 115 us  [per_device(): pl.pallas_call(kernel, out_shape=(jax.ShapeDtypeStruct((2, 2, 128, 256),...]
where the time goes in v3:
time: 118 us
  Pallas kernels  115 us (97%)
  local copies, waits for them, and re-layouts  2.44 us (2%)
    pallas_call x1, Pallas kernels, per_device(): pl.pallas_call(kernel, out_shape=(jax.ShapeDtypeStruct((2, 2, 128, 256),...  115 us
    unnamed x4, local copies, waits for them, and re-layouts  2.44 us

profile of v3, /device:TPU:1, one launch (start us, length us, event | category | flops | bytes accessed | tf_op | source)
XLA Modules:
  0.0 118.0 jit_solution(9913529291594702682)
XLA Ops:
  0.6 114.9 %whole.1 = (f32[2,2,128,256]{3,2,1,0:T(8,128)}, f32[2,2]{1,0:T(2,128)}) custom-call(bf16[2,2,128,256]{3,2,1,0:T(8,128)(2,1)} %tr.1, f32[2,2]{1,0:T(2,128)} %wave.1, f32[32,2048]{1,0:T(8,128)} %constant.16.clone.base_c, f32[32,2048]{1,0:T(8,128)} %constant.17.clone.base_s, f32[16,2048]{1,0:T(8,128)} %constant.18.clone.mul_c, ...), custom_call_target="tpu_custom_call" | custom-call | tf_op jit(solution)/shard_map/whole/pallas_call | solution.py:591
  115.5 0.0 copy-start
  115.5 1.9 %copy.14 = f32[2,2,128,256]{3,2,1,0:T(8,128)} copy(f32[2,2,128,256]{3,2,1,0:T(8,128)} %get-tuple-element.4) | data formatting | bytes 1048576
  117.4 0.0 copy-done
  117.4 0.6 copy.15
Async XLA Ops:
  115.5 1.9 %copy-start = (f32[2,2]{1,0:T(2,128)S(1)}, f32[2,2]{1,0:T(2,128)}, u32[]{:S(2)}) copy-start(f32[2,2]{1,0:T(2,128)} %get-tuple-element.5) | copy-start | bytes 52

commit v4 on v3

--- a/solution.py
+++ b/solution.py
@@ -157,6 +157,28 @@
     def _():
         arrived(tf.at[:, own_rows, 256:512], swap + 1)
 
+    root = 1.0 / math.sqrt(N)
+    wr = wave[c, 0] * root
+    wi = wave[c, 1] * root
+
+    def dot(a, b):
+        return lax.dot_general(a, b, (((1,), (0,)), ((), ())), preferred_element_type=F32)
+
+    def dot_nt(a, b):
+        return lax.dot_general(a, b, (((1,), (1,)), ((), ())), preferred_element_type=F32)
+
+    def back_rows(n):
+        errors = mf[...].reshape(256, 512)
+        here = ds(n * 512, 512, 512)
+        a, b = dot_nt(tf[0, here, :], errors), dot_nt(tf[1, here, :], errors)
+        br, bi = a[:, :128] + b[:, 128:], a[:, 128:] - b[:, :128]
+        pg[0, here, :] = -(wr * br + wi * bi)
+        pg[1, here, :] = -(wr * bi - wi * br)
+
+    def back_start():
+        for part in range(2):
+            mf[part] = tf[part, own_rows, :]
+
     def shift(at, axis, d):
         zz_, xx_ = at
         return ((zz_ + d + 4) % 4, xx_) if axis == 0 else (zz_, (xx_ + d + 4) % 4)
@@ -166,12 +188,10 @@
         return dev(a * 4 + b, g)
 
     def block(at, kind, part=None):
-        start = (at[0] * 4 + at[1]) * 128 + 96 * kind
-        rows = 32 if kind else 96
+        start = (at[0] * 4 + at[1]) * 128 + 32 * kind
         if part is not None:
-            rows = rows // 2
-            start = start + rows * part
-        return tf.at[:, ds(start, rows, 16), :]
+            return tf.at[:, ds(start + 16 * part, 16, 16), :]
+        return tf.at[:, ds(start, 32, 16), :]
 
     def ag_start(at, axis, half):
         s_id = ids(4)
@@ -217,39 +237,50 @@
 
     mark("gather_a")
     home = (z, lane2)
-    first = [ag_start(home, 0, 0), ag_start(home, 1, 1)]
-    second = [ag_start(home, 1, 0), ag_start(home, 0, 1)]
-    make_table(0, 12)
+    kinds = (0, 1, 2, 3)
+    first_axis = (0, 0, 0, 1)
+    first = [ag_start(home, first_axis[k], k) for k in kinds]
+    own = [ag_start(home, 1 - first_axis[k], k) for k in kinds]
+    make_table(0, 16)
+    make_order()
     mark("gather_b")
-    for item in first:
-        ag_forward(item)
-    for d in (-1, 1):
-        second.append(ag_start(shift(home, 0, d), 1, 0))
-        second.append(ag_start(shift(home, 1, d), 0, 1))
-    mark("table_b")
-    make_table(12, 16)
-    make_order()
+    near = {}
+
+    def pass_on(k, hops):
+        near[k, hops] = [ag_start(shift(home, first_axis[k], d), 1 - first_axis[k], k) for d in hops]
+
+    for k in (3, 0, 1, 2):
+        ag_forward(first[k])
+        pass_on(k, (-1, 1))
+        if k < 3:
+            ag_forward(own[k])
+    ag_forward(own[3])
+    for k in kinds:
+        ag_finish(first[k])
+        pass_on(k, (2,))
     mark("gather_c")
-    for item in second[:2]:
-        ag_forward(item)
-    for item in first:
-        ag_finish(item)
-    second.append(ag_start(shift(home, 0, 2), 1, 0))
-    second.append(ag_start(shift(home, 1, 2), 0, 1))
-    for item in second[2:]:
-        ag_forward(item)
-    for item in second:
-        ag_finish(item)
-
-    root = 1.0 / math.sqrt(N)
-    wr = wave[c, 0] * root
-    wi = wave[c, 1] * root
-
-    def dot(a, b):
-        return lax.dot_general(a, b, (((1,), (0,)), ((), ())), preferred_element_type=F32)
-
-    def dot_nt(a, b):
-        return lax.dot_general(a, b, (((1,), (1,)), ((), ())), preferred_element_type=F32)
+    for k in kinds:
+        for item in near[k, (-1, 1)]:
+            ag_forward(item)
+    for k in kinds:
+        ag_finish(own[k])
+    mark("gather_back")
+    back_start()
+    back_rows(z)
+    mark("gather_d")
+    for k in kinds:
+        ag_forward(near[k, (2,)][0])
+    for k in kinds:
+        for item in near[k, (-1, 1)]:
+            ag_finish(item)
+    mark("gather_back")
+    back_rows((z + 3) % 4)
+    back_rows((z + 1) % 4)
+    mark("gather_e")
+    for k in kinds:
+        ag_finish(near[k, (2,)][0])
+    mark("gather_back")
+    back_rows((z + 2) % 4)
 
     def quarters(load, ub):
         x = [[load(part, q) for part in range(2)] for q in range(4)]
@@ -290,28 +321,28 @@
     def residue(ref, q):
         return ref.at[:, q % 4, ds(32 * (q // 4), 32, 32), :]
 
+    offsets = [(a, b) for a in range(4) for b in range(4) if a or b]
+    offsets.sort(key=lambda o: -(min(o[0], 4 - o[0]) + min(o[1], 4 - o[1])))
+
+    def place(a, b):
+        return (z + a) % 4 * 4 + (lane2 + b) % 4
+
     def plane_exchange(source, landing, first_id):
-        @pl.loop(1, 16)
-        def _(k):
-            q = (p + k) % 16
+        for k, (a, b) in enumerate(offsets):
+            q = place(a, b)
             rcopy(source(q), landing(p), first_id + k, first_id + k, dev(q, g)).start()
 
     def plane_wait(source, landing, first_id):
-        @pl.loop(1, 16)
-        def _(k):
-            q = (p + 16 - k) % 16
-            w = rcopy(source((p + k) % 16), landing(q), first_id + k, first_id + k, dev(q, g))
+        for k, (a, b) in reversed(list(enumerate(offsets))):
+            q = place(4 - a, 4 - b)
+            w = rcopy(source(place(a, b)), landing(q), first_id + k, first_id + k, dev(q, g))
             w.wait_recv()
             w.wait_send()
 
     totals = []
     for it in range(2):
         if it == 0:
-            re = tf[0, own_rows, :]
-            im = tf[1, own_rows, :]
-            mf[0] = re
-            mf[1] = im
-            ref, imf = re.astype(F32), im.astype(F32)
+            ref, imf = mf[0].astype(F32), mf[1].astype(F32)
             squares = jnp.sum(ref * ref + imf * imf)
         else:
             mark("g_left")
@@ -332,22 +363,28 @@
                 for r in range(4):
                     hh[part, r, :, ds(128 * g, 128, 128)] = wt[part, r].astype(F32).T.astype(BF)
             mark("g_gather")
-            gid = ids(4)
-
-            def col_block(yy, rows=None):
-                if rows is None:
-                    return hh.at[:, :, :, ds(128 * yy, 128, 128)]
-                return hh.at[rows, :, :, ds(128 * yy, 128, 128)]
+            gid = ids(10)
+
+            def held(gg, part, h=None):
+                which = slice(None) if h is None else pl.ds(2 * h, 2)
+                return hh.at[part, which, :, ds(128 * gg, 128, 128)]
 
             up, down, far = (g + 1) % 4, (g + 3) % 4, (g + 2) % 4
-            send(col_block(g), col_block(g), gid, dev(p, up))
-            send(col_block(g), col_block(g), gid + 1, dev(p, down))
-            arrived(col_block(down), gid)
-            send(col_block(down, 0), col_block(down, 0), gid + 2, dev(p, up))
-            arrived(col_block(up), gid + 1)
-            send(col_block(up, 1), col_block(up, 1), gid + 3, dev(p, down))
-            arrived(col_block(far, 0), gid + 2)
-            arrived(col_block(far, 1), gid + 3)
+            for h in range(2):
+                send(held(g, 0, h), held(g, 0, h), gid + h, dev(p, up))
+                send(held(g, 1, h), held(g, 1, h), gid + 2 + h, dev(p, down))
+            send(held(g, 1), held(g, 1), gid + 4, dev(p, up))
+            send(held(g, 0), held(g, 0), gid + 5, dev(p, down))
+            for h in range(2):
+                arrived(held(down, 0, h), gid + h)
+                send(held(down, 0, h), held(down, 0, h), gid + 6 + h, dev(p, up))
+                arrived(held(up, 1, h), gid + 2 + h)
+                send(held(up, 1, h), held(up, 1, h), gid + 8 + h, dev(p, down))
+            arrived(held(down, 1), gid + 4)
+            arrived(held(up, 0), gid + 5)
+            for h in range(2):
+                arrived(held(far, 0, h), gid + 6 + h)
+                arrived(held(far, 1, h), gid + 8 + h)
 
             mark("g_right")
             def put_model(col, a, b):
@@ -372,15 +409,12 @@
                 mf[0, :, n * 256 : n * 256 + 256] = mr.astype(BF)
                 mf[1, :, n * 256 : n * 256 + 256] = mi.astype(BF)
 
-        mark("back")
-        @pl.loop(0, 4)
-        def _(n):
-            errors = mf[...].reshape(256, 512)
-            here = ds(n * 512, 512, 512)
-            a, b = dot_nt(tf[0, here, :], errors), dot_nt(tf[1, here, :], errors)
-            br, bi = a[:, :128] + b[:, 128:], a[:, 128:] - b[:, :128]
-            pg[0, here, :] = -(wr * br + wi * bi)
-            pg[1, here, :] = -(wr * bi - wi * br)
+        if it:
+            mark("back")
+
+            @pl.loop(0, 4)
+            def _(n):
+                back_rows(n)
 
         mine = ds(512 * g, 512, 512)
         for part in range(2):
@@ -391,6 +425,15 @@
             lambda part, q: pg[part, q * QUARTER : q * QUARTER + QUARTER, :],
             lambda r, part: ubt.at[r, :, pl.ds(128 * part, 128)],
         )
+        up, down, far = (g + 1) % 4, (g + 3) % 4, (g + 2) % 4
+        rid = ids(12)
+
+        def piece(ref, gg, h, part):
+            return ref.at[it, part, pl.ds(2 * h, 2), ds(128 * gg, 128, 128), :]
+
+        def slot(ref, h, *part):
+            return ref.at[(it, *part, pl.ds(2 * h, 2))]
+
         for r in range(4):
             there = pl.ds(r * QUARTER, QUARTER)
             a, b = dot(inv_c[there, :], ubt[r]), dot(inv_s[there, :], ubt[r])
@@ -399,26 +442,32 @@
             tp[1, r] = ti_
             sb[it, 0, r] = tr_.astype(BF)
             sb[it, 1, r] = ti_.astype(BF)
+            if r % 2:
+                h = r // 2
+                send(piece(sb, far, h, 0), slot(ra, h), rid + h, dev(p, up))
+                send(piece(sb, far, h, 1), slot(rb, h), rid + 2 + h, dev(p, down))
 
         mark("scatter")
-        up, down, far = (g + 1) % 4, (g + 3) % 4, (g + 2) % 4
-        cols_of = lambda gg: ds(128 * gg, 128, 128)
-        rid = ids(6)
-        send(sb.at[it, 0, :, cols_of(far), :], ra.at[it], rid, dev(p, up))
-        send(sb.at[it, 1, :, cols_of(far), :], rb.at[it], rid + 1, dev(p, down))
-        send(sb.at[it, 1, :, cols_of(up), :], dl.at[it, 1], rid + 2, dev(p, up))
-        send(sb.at[it, 0, :, cols_of(down), :], dr.at[it, 0], rid + 3, dev(p, down))
-        arrived(ra.at[it], rid)
-        qa[it] = (tp[0, :, cols_of(up), :] + ra[it].astype(F32)).astype(BF)
-        send(qa.at[it], dl.at[it, 0], rid + 4, dev(p, up))
-        arrived(rb.at[it], rid + 1)
-        qb[it] = (tp[1, :, cols_of(down), :] + rb[it].astype(F32)).astype(BF)
-        send(qb.at[it], dr.at[it, 1], rid + 5, dev(p, down))
-        arrived(dl.at[it, 1], rid + 2)
-        arrived(dr.at[it, 0], rid + 3)
-        arrived(dl.at[it, 0], rid + 4)
-        arrived(dr.at[it, 1], rid + 5)
-        zt[it] = (tp[:, :, cols_of(g), :] + dl[it].astype(F32) + dr[it].astype(F32)).astype(BF)
+        for h in range(2):
+            send(piece(sb, up, h, 1), slot(dl, h, 1), rid + 4 + h, dev(p, up))
+            send(piece(sb, down, h, 0), slot(dr, h, 0), rid + 6 + h, dev(p, down))
+        for h in range(2):
+            pair = pl.ds(2 * h, 2)
+            arrived(slot(ra, h), rid + h)
+            qa[it, pair] = (tp[0, pair, ds(128 * up, 128, 128), :] + ra[it, pair].astype(F32)).astype(BF)
+            send(slot(qa, h), slot(dl, h, 0), rid + 8 + h, dev(p, up))
+            arrived(slot(rb, h), rid + 2 + h)
+            qb[it, pair] = (tp[1, pair, ds(128 * down, 128, 128), :] + rb[it, pair].astype(F32)).astype(BF)
+            send(slot(qb, h), slot(dr, h, 1), rid + 10 + h, dev(p, down))
+        for h in range(2):
+            arrived(slot(dl, h, 1), rid + 4 + h)
+            arrived(slot(dr, h, 0), rid + 6 + h)
+        for h in range(2):
+            pair = pl.ds(2 * h, 2)
+            arrived(slot(dl, h, 0), rid + 8 + h)
+            arrived(slot(dr, h, 1), rid + 10 + h)
+            total = tp[:, pair, ds(128 * g, 128, 128), :] + dl[it, :, pair].astype(F32)
+            zt[it, :, pair] = (total + dr[it, :, pair].astype(F32)).astype(BF)
         mark("f_plane")
         xid = ids(16)
         src_of = lambda q: residue(zt.at[it], q)
@@ -471,9 +520,8 @@
                 s_id = oid + (q + 16 - p) % 16
                 return rcopy(out_src(q), out_dst(p), s_id, oid + p, chip(q // 4, q % 4, g, c))
 
-            @pl.loop(1, 16)
-            def _(k):
-                out_copy((p + k) % 16).start()
+            for a, b in offsets:
+                out_copy(place(a, b)).start()
 
             @pl.when(away)
             def _():
@@ -568,7 +616,7 @@
 
 def scratch():
     v = lambda *shape, t=BF: pltpu.VMEM(shape, t)
-    pair = pltpu.SemaphoreType.DMA((192,))
+    pair = pltpu.SemaphoreType.DMA((320,))
     return [
         v(2, N, 512), v(QUARTER, N), v(QUARTER, N), v(N, QUARTER), v(N, QUARTER), v(512, 512),
         v(2, N, 128, t=F32), v(4, QUARTER, 256), v(2, 4, QUARTER, 128, t=F32),

time: 118 us -> 112 us (0.949)
  Pallas kernels: 115 us -> 109 us
    pallas_call x1, Pallas kernels: 115 us -> 109 us  [per_device(): pl.pallas_call(kernel, out_shape=(jax.ShapeDtypeStruct((2, 2, 128, 256),...]
where the time goes in v4:
time: 112 us
  Pallas kernels  109 us (97%)
  local copies, waits for them, and re-layouts  2.44 us (2%)
    pallas_call x1, Pallas kernels, per_device(): pl.pallas_call(kernel, out_shape=(jax.ShapeDtypeStruct((2, 2, 128, 256),...  109 us
    unnamed x4, local copies, waits for them, and re-layouts  2.44 us

profile of v4, /device:TPU:1, one launch (start us, length us, event | category | flops | bytes accessed | tf_op | source)
XLA Modules:
  0.0 111.8 jit_solution(5358485366109325593)
XLA Ops:
  0.6 108.7 %whole.1 = (f32[2,2,128,256]{3,2,1,0:T(8,128)}, f32[2,2]{1,0:T(2,128)}) custom-call(bf16[2,2,128,256]{3,2,1,0:T(8,128)(2,1)} %tr.1, f32[2,2]{1,0:T(2,128)} %wave.1, f32[32,2048]{1,0:T(8,128)} %constant.16.clone.base_c, f32[32,2048]{1,0:T(8,128)} %constant.17.clone.base_s, f32[16,2048]{1,0:T(8,128)} %constant.18.clone.mul_c, ...), custom_call_target="tpu_custom_call" | custom-call | tf_op jit(solution)/shard_map/whole/pallas_call | solution.py:639
  109.4 0.0 copy-start
  109.4 1.9 %copy.14 = f32[2,2,128,256]{3,2,1,0:T(8,128)} copy(f32[2,2,128,256]{3,2,1,0:T(8,128)} %get-tuple-element.4) | data formatting | bytes 1048576
  111.3 0.0 copy-done
  111.3 0.6 copy.15
Async XLA Ops:
  109.4 1.9 %copy-start = (f32[2,2]{1,0:T(2,128)S(1)}, f32[2,2]{1,0:T(2,128)}, u32[]{:S(2)}) copy-start(f32[2,2]{1,0:T(2,128)} %get-tuple-element.5) | copy-start | bytes 52

commit v5 on v4

--- a/solution.py
+++ b/solution.py
@@ -12,6 +12,8 @@
 MESH = pl.DeviceIdType.MESH
 N = 2048
 BASE = 32
+RECEIVES = 92
+SENDS = 16
 QUARTER = N // 4
 STEP = 0.4
 SHRINK = 0.2
@@ -37,11 +39,14 @@
 
 
 def kernel(
-    tr, wave, base_c, base_s, mul_c, mul_s, ibase_c, ibase_s, imul_c, imul_s, out, norms,
+    tr_any, wave, t0, t1, t2, t3, t4, t5, t6, t7, out, norms,
+    tr, b0, b1, b2, b3, b4, b5, b6, b7,
     tf, tab_c, tab_s, inv_c, inv_s, perm, pg, ubt, tp, sb, ra, rb, qa, qb, dl, dr, ub, zt, xt,
     trial, cfo, cb, hb, wt, hh, mb, mf, ot, nat, keep, got, st1, st2, sr1, sr2, nt, nr,
-    ssem, rsem,
+    ssem, rsem, lsem,
 ):
+    tables_any = (t0, t1, t2, t3, t4, t5, t6, t7)
+    tables = (b0, b1, b2, b3, b4, b5, b6, b7)
     src = lax.axis_index("src")
     rcv = lax.axis_index("rcv")
     y = rcv // 2
@@ -51,7 +56,7 @@
     lane2 = (1 - c) * x + c * y
     g = (1 - c) * y + c * x
     p = z * 4 + lane2
-    used = [0]
+    used = [0, 0]
     pending = []
 
     stage = [None]
@@ -67,6 +72,10 @@
         used[0] += n
         return used[0] - n
 
+    def out_id():
+        used[1] += 1
+        return used[1] - 1
+
     def chip(zz_, xx_, yy_, cc_):
         return (zz_ * 4 + xx_, yy_ * 2 + cc_)
 
@@ -82,23 +91,26 @@
             device_id=where, device_id_type=MESH,
         )
 
-    def send(src, dst, s_id, where):
-        copy = rcopy(src, dst, s_id, s_id, where)
-        copy.start()
-        pending.append(copy)
+    def send(src, dst, s_id, r_id, where):
+        rcopy(src, dst, s_id, r_id, where).start()
 
     def arrived(ref, r_id):
-        rcopy(ref, ref, r_id, r_id, partner).wait_recv()
-
-    def sent():
-        for copy in pending:
-            copy.wait_send()
-        pending.clear()
+        rcopy(ref, ref, 0, r_id, partner).wait_recv()
+
+    def sent(ref, s_id):
+        pending.append(rcopy(ref, ref, s_id, 0, partner))
 
     def ds(start, size, unit):
         return pl.ds(pl.multiple_of(start, unit), size)
 
     mark("entry")
+    fetched = [
+        pltpu.make_async_copy(a, b, lsem.at[k])
+        for k, (a, b) in enumerate(zip((tr_any, *tables_any), (tr, *tables)))
+    ]
+    for copy in fetched:
+        copy.start()
+    base_c, base_s, mul_c, mul_s, ibase_c, ibase_s, imul_c, imul_s = tables
     barrier = pltpu.get_barrier_semaphore()
 
     def greet(where):
@@ -127,10 +139,11 @@
 
     mark("swap")
     own_rows = ds(128 * p, 128, 128)
-    swap = ids(2)
+    fetched[0].wait()
+    swap, swap_s = ids(2), [out_id(), out_id()]
     landing = tf.at[:, ds(128 * src, 128, 128), ds(256 * c, 256, 256)]
-    to_first = rcopy(tr.at[0], landing, swap, swap + c, chip(z, x, y, 0))
-    to_second = rcopy(tr.at[1], landing, swap + 1, swap + c, chip(z, y, x, 1))
+    to_first = rcopy(tr.at[0], landing, swap_s[0], swap + c, chip(z, x, y, 0))
+    to_second = rcopy(tr.at[1], landing, swap_s[1], swap + c, chip(z, y, x, 1))
     stays = jnp.logical_and(c == 1, x == y)
 
     @pl.when(jnp.logical_not(stays))
@@ -193,25 +206,25 @@
             return tf.at[:, ds(start + 16 * part, 16, 16), :]
         return tf.at[:, ds(start, 32, 16), :]
 
+    gather_s = out_id()
+
     def ag_start(at, axis, half):
-        s_id = ids(4)
-        send(block(at, half), block(at, half), s_id, neighbour(axis, 1))
-        send(block(at, half), block(at, half), s_id + 1, neighbour(axis, -1))
-        return at, axis, half, s_id
+        r_id = ids(3)
+        send(block(at, half), block(at, half), gather_s, r_id, neighbour(axis, 1))
+        send(block(at, half), block(at, half), gather_s, r_id + 1, neighbour(axis, -1))
+        return at, axis, half, r_id
 
     def ag_forward(item):
-        at, axis, half, s_id = item
+        at, axis, half, r_id = item
         left, right = shift(at, axis, -1), shift(at, axis, 1)
-        arrived(block(left, half), s_id)
-        send(block(left, half, 0), block(left, half, 0), s_id + 2, neighbour(axis, 1))
-        arrived(block(right, half), s_id + 1)
-        send(block(right, half, 1), block(right, half, 1), s_id + 3, neighbour(axis, -1))
+        arrived(block(left, half), r_id)
+        send(block(left, half, 0), block(left, half, 0), gather_s, r_id + 2, neighbour(axis, 1))
+        arrived(block(right, half), r_id + 1)
+        send(block(right, half, 1), block(right, half, 1), gather_s, r_id + 2, neighbour(axis, -1))
 
     def ag_finish(item):
-        at, axis, half, s_id = item
-        far = shift(at, axis, 2)
-        arrived(block(far, half, 0), s_id + 2)
-        arrived(block(far, half, 1), s_id + 3)
+        at, axis, half, r_id = item
+        arrived(block(shift(at, axis, 2), half), r_id + 2)
 
     def make_table(first, last):
         @pl.loop(first, last)
@@ -240,7 +253,9 @@
     kinds = (0, 1, 2, 3)
     first_axis = (0, 0, 0, 1)
     first = [ag_start(home, first_axis[k], k) for k in kinds]
-    own = [ag_start(home, 1 - first_axis[k], k) for k in kinds]
+    own = [ag_start(home, 1, k) for k in (0, 1, 2)]
+    for copy in fetched[1:]:
+        copy.wait()
     make_table(0, 16)
     make_order()
     mark("gather_b")
@@ -249,15 +264,20 @@
     def pass_on(k, hops):
         near[k, hops] = [ag_start(shift(home, first_axis[k], d), 1 - first_axis[k], k) for d in hops]
 
-    for k in (3, 0, 1, 2):
+    ag_forward(first[3])
+    for k in (0, 1, 2):
         ag_forward(first[k])
         pass_on(k, (-1, 1))
-        if k < 3:
-            ag_forward(own[k])
-    ag_forward(own[3])
-    for k in kinds:
+        if k == 2:
+            own.append(ag_start(home, 0, 3))
+        ag_forward(own[k])
+    pass_on(3, (-1, 1))
+    ag_finish(first[3])
+    for k in (0, 1, 2):
         ag_finish(first[k])
         pass_on(k, (2,))
+    pass_on(3, (2,))
+    ag_forward(own[3])
     mark("gather_c")
     for k in kinds:
         for item in near[k, (-1, 1)]:
@@ -279,6 +299,7 @@
     mark("gather_e")
     for k in kinds:
         ag_finish(near[k, (2,)][0])
+    sent(tf.at[:, 0:1920, :], gather_s)
     mark("gather_back")
     back_rows((z + 2) % 4)
 
@@ -327,17 +348,14 @@
     def place(a, b):
         return (z + a) % 4 * 4 + (lane2 + b) % 4
 
-    def plane_exchange(source, landing, first_id):
-        for k, (a, b) in enumerate(offsets):
+    def plane_exchange(source, landing, r_id, s_id):
+        for a, b in offsets:
             q = place(a, b)
-            rcopy(source(q), landing(p), first_id + k, first_id + k, dev(q, g)).start()
-
-    def plane_wait(source, landing, first_id):
-        for k, (a, b) in reversed(list(enumerate(offsets))):
-            q = place(4 - a, 4 - b)
-            w = rcopy(source(place(a, b)), landing(q), first_id + k, first_id + k, dev(q, g))
-            w.wait_recv()
-            w.wait_send()
+            rcopy(source(q), landing(p), s_id, r_id, dev(q, g)).start()
+
+    def plane_wait(others, r_id, s_id):
+        arrived(others, r_id)
+        sent(others, s_id)
 
     totals = []
     for it in range(2):
@@ -353,38 +371,42 @@
             inverse(lambda r: cb[:, r].reshape(64, QUARTER), 32, put_half)
 
             mark("g_plane")
-            wid = ids(16)
+            wid, wid_s = ids(1), out_id()
             src_of = lambda q: hb.at[:, :, ds(128 * q, 128, 128)]
             dst_of = lambda q: residue(wt, q)
-            plane_exchange(src_of, dst_of, wid)
+            plane_exchange(src_of, dst_of, wid, wid_s)
             residue(wt, p)[...] = hb[:, :, ds(128 * p, 128, 128)]
-            plane_wait(src_of, dst_of, wid)
+            plane_wait(hb.at[:, :, 0:1920], wid, wid_s)
             for part in range(2):
                 for r in range(4):
                     hh[part, r, :, ds(128 * g, 128, 128)] = wt[part, r].astype(F32).T.astype(BF)
             mark("g_gather")
-            gid = ids(10)
+            gid, gid_s = ids(8), out_id()
 
             def held(gg, part, h=None):
                 which = slice(None) if h is None else pl.ds(2 * h, 2)
                 return hh.at[part, which, :, ds(128 * gg, 128, 128)]
 
             up, down, far = (g + 1) % 4, (g + 3) % 4, (g + 2) % 4
+
+            def pass_held(gg, part, h, r_id, to):
+                send(held(gg, part, h), held(gg, part, h), gid_s, gid + r_id, dev(p, to))
+
             for h in range(2):
-                send(held(g, 0, h), held(g, 0, h), gid + h, dev(p, up))
-                send(held(g, 1, h), held(g, 1, h), gid + 2 + h, dev(p, down))
-            send(held(g, 1), held(g, 1), gid + 4, dev(p, up))
-            send(held(g, 0), held(g, 0), gid + 5, dev(p, down))
+                pass_held(g, 0, h, h, up)
+                pass_held(g, 1, h, 2 + h, down)
+            pass_held(g, 1, None, 4, up)
+            pass_held(g, 0, None, 5, down)
             for h in range(2):
                 arrived(held(down, 0, h), gid + h)
-                send(held(down, 0, h), held(down, 0, h), gid + 6 + h, dev(p, up))
+                pass_held(down, 0, h, 6, up)
                 arrived(held(up, 1, h), gid + 2 + h)
-                send(held(up, 1, h), held(up, 1, h), gid + 8 + h, dev(p, down))
+                pass_held(up, 1, h, 7, down)
             arrived(held(down, 1), gid + 4)
             arrived(held(up, 0), gid + 5)
-            for h in range(2):
-                arrived(held(far, 0, h), gid + 6 + h)
-                arrived(held(far, 1, h), gid + 8 + h)
+            arrived(held(far, 0), gid + 6)
+            arrived(held(far, 1), gid + 7)
+            sent(hh.at[:, 0:3], gid_s)
 
             mark("g_right")
             def put_model(col, a, b):
@@ -426,7 +448,7 @@
             lambda r, part: ubt.at[r, :, pl.ds(128 * part, 128)],
         )
         up, down, far = (g + 1) % 4, (g + 3) % 4, (g + 2) % 4
-        rid = ids(12)
+        rid, rid_s = ids(6), out_id()
 
         def piece(ref, gg, h, part):
             return ref.at[it, part, pl.ds(2 * h, 2), ds(128 * gg, 128, 128), :]
@@ -444,37 +466,33 @@
             sb[it, 1, r] = ti_.astype(BF)
             if r % 2:
                 h = r // 2
-                send(piece(sb, far, h, 0), slot(ra, h), rid + h, dev(p, up))
-                send(piece(sb, far, h, 1), slot(rb, h), rid + 2 + h, dev(p, down))
+                send(piece(sb, far, h, 0), slot(ra, h), rid_s, rid + h, dev(p, up))
+                send(piece(sb, far, h, 1), slot(rb, h), rid_s, rid + 2 + h, dev(p, down))
 
         mark("scatter")
         for h in range(2):
-            send(piece(sb, up, h, 1), slot(dl, h, 1), rid + 4 + h, dev(p, up))
-            send(piece(sb, down, h, 0), slot(dr, h, 0), rid + 6 + h, dev(p, down))
+            send(piece(sb, up, h, 1), slot(dl, h, 1), rid_s, rid + 4, dev(p, up))
+            send(piece(sb, down, h, 0), slot(dr, h, 0), rid_s, rid + 5, dev(p, down))
         for h in range(2):
             pair = pl.ds(2 * h, 2)
             arrived(slot(ra, h), rid + h)
             qa[it, pair] = (tp[0, pair, ds(128 * up, 128, 128), :] + ra[it, pair].astype(F32)).astype(BF)
-            send(slot(qa, h), slot(dl, h, 0), rid + 8 + h, dev(p, up))
+            send(slot(qa, h), slot(dl, h, 0), rid_s, rid + 4, dev(p, up))
             arrived(slot(rb, h), rid + 2 + h)
             qb[it, pair] = (tp[1, pair, ds(128 * down, 128, 128), :] + rb[it, pair].astype(F32)).astype(BF)
-            send(slot(qb, h), slot(dr, h, 1), rid + 10 + h, dev(p, down))
-        for h in range(2):
-            arrived(slot(dl, h, 1), rid + 4 + h)
-            arrived(slot(dr, h, 0), rid + 6 + h)
-        for h in range(2):
-            pair = pl.ds(2 * h, 2)
-            arrived(slot(dl, h, 0), rid + 8 + h)
-            arrived(slot(dr, h, 1), rid + 10 + h)
-            total = tp[:, pair, ds(128 * g, 128, 128), :] + dl[it, :, pair].astype(F32)
-            zt[it, :, pair] = (total + dr[it, :, pair].astype(F32)).astype(BF)
+            send(slot(qb, h), slot(dr, h, 1), rid_s, rid + 5, dev(p, down))
+        arrived(dl.at[it], rid + 4)
+        arrived(dr.at[it], rid + 5)
+        sent(sb.at[it, :, 0:3], rid_s)
+        total = tp[:, :, ds(128 * g, 128, 128), :] + dl[it].astype(F32)
+        zt[it] = (total + dr[it].astype(F32)).astype(BF)
         mark("f_plane")
-        xid = ids(16)
+        xid, xid_s = ids(1), out_id()
         src_of = lambda q: residue(zt.at[it], q)
         dst_of = lambda q: xt.at[it, :, :, ds(128 * q, 128, 128)]
-        plane_exchange(src_of, dst_of, xid)
+        plane_exchange(src_of, dst_of, xid, xid_s)
         dst_of(p)[...] = src_of(p)[...]
-        plane_wait(src_of, dst_of, xid)
+        plane_wait(xt.at[it, :, :, 0:1920], xid, xid_s)
 
         mark("f_left")
         peaks = []
@@ -493,14 +511,14 @@
         mark("stats")
         lane = lax.broadcasted_iota(jnp.int32, (1, 128), 1)
         st1[it] = jnp.where(lane < 64, peak, squares)
-        sid = ids(16)
+        sid, sid_s = ids(1), out_id()
         src_of = lambda q: st1.at[it]
         dst_of = lambda q: sr1.at[it, q]
-        plane_exchange(src_of, dst_of, sid)
+        plane_exchange(src_of, dst_of, sid, sid_s)
         sr1[it, p] = st1[it]
         if it:
             mark("out_send")
-            oid = ids(16)
+            oid, oid_s = ids(1), out_id()
             for b in range(4):
                 v = [trial[part, r, :, 128 * b : 128 * b + 128] for r in range(4) for part in range(2)]
                 v = jnp.concatenate([jnp.concatenate(v[k::2], axis=1) for k in range(2)], axis=0)
@@ -517,8 +535,7 @@
             away = jnp.logical_and(c == 1, x != y)
 
             def out_copy(q):
-                s_id = oid + (q + 16 - p) % 16
-                return rcopy(out_src(q), out_dst(p), s_id, oid + p, chip(q // 4, q % 4, g, c))
+                return rcopy(out_src(q), out_dst(p), oid_s, oid, chip(q // 4, q % 4, g, c))
 
             for a, b in offsets:
                 out_copy(place(a, b)).start()
@@ -532,17 +549,17 @@
                 out_dst(p)[...] = out_src(p)[...]
 
             mark("stats_wait")
-        plane_wait(src_of, dst_of, sid)
+        plane_wait(sr1.at[it, 0:15], sid, sid_s)
         def joined(all_of):
             return jnp.where(lane < 64, jnp.max(all_of, axis=0), jnp.sum(all_of, axis=0))
 
         st2[it] = joined(sr1[it])
-        tid = ids(4)
-        for d in (1, 2, 3):
-            send(st2.at[it], sr2.at[it, g], tid + d, dev(p, (g + d) % 4))
+        tid, tid_s = ids(1), out_id()
+        for d in (2, 1, 3):
+            send(st2.at[it], sr2.at[it, g], tid_s, tid, dev(p, (g + d) % 4))
         sr2[it, g] = st2[it]
-        for d in (1, 2, 3):
-            arrived(sr2.at[it, (g + 4 - d) % 4], tid + d)
+        arrived(sr2.at[it, 0:3], tid)
+        sent(sr2.at[it, 0:3], tid_s)
         both = joined(sr2[it])
         totals.append(jnp.max(jnp.where(lane < 64, 0.0, both)))
         mark("shrink")
@@ -562,21 +579,18 @@
                 cb[1, r] = b.astype(BF)
 
     mark("out_wait")
-    nid = ids(1)
+    nid, nid_s = ids(1), out_id()
     for it in range(2):
         nt[it] = jnp.sqrt(jnp.full((1, 128), totals[it], F32))
-    send(nt, nr, nid, partner)
-
-    @pl.loop(1, 16)
-    def _(k):
-        q = (p + k) % 16
-        arrived(out_dst(q), oid + q)
-        out_copy(q).wait_send()
+    send(nt, nr, nid_s, nid, partner)
 
     @pl.when(away)
     def _():
-        arrived(out_dst(p), oid + p)
-        out_copy(p).wait_send()
+        rcopy(ot, ot, oid_s, oid, partner).wait_recv()
+
+    @pl.when(jnp.logical_not(away))
+    def _():
+        rcopy(ot.at[:, 0:15], ot.at[:, 0:15], oid_s, oid, partner).wait_recv()
 
     mark("out_turn")
     for b in range(4):
@@ -584,14 +598,14 @@
             a, d = shrunk(ot[0, 4 * b + r], ot[1, 4 * b + r])
             nat[0, b, pl.ds(r, 32, stride=4), :] = a
             nat[1, b, pl.ds(r, 32, stride=4), :] = d
-    halves = ids(2)
+    halves, halves_s = ids(1), out_id()
 
     def turned(part, half):
         return jnp.concatenate([nat[part, 2 * half + k].T for k in range(2)], axis=1)
 
     for part in range(2):
         keep[part] = turned(part, 1 - c)
-    send(keep, got, halves, partner)
+    send(keep, got, halves_s, halves, partner)
     for part in range(2):
         out[c, part] = turned(part, c)
     mark("out_swap")
@@ -601,7 +615,18 @@
         norms[it, 1 - c] = jnp.max(nr[it])
     arrived(got, halves)
     out[1 - c] = got[...]
-    sent()
+    for copy in pending:
+        copy.wait_send()
+    rcopy(nt, nt, nid_s, nid, partner).wait_send()
+    rcopy(keep, keep, halves_s, halves, partner).wait_send()
+
+    @pl.when(away)
+    def _():
+        rcopy(ot, ot, oid_s, oid, partner).wait_send()
+
+    @pl.when(jnp.logical_not(away))
+    def _():
+        rcopy(ot.at[:, 0:15], ot.at[:, 0:15], oid_s, oid, partner).wait_send()
 
     @pl.when(jnp.logical_not(stays))
     def _():
@@ -611,13 +636,14 @@
     def _():
         to_first.wait_send()
 
+    assert used == [RECEIVES, SENDS], used
     mark(None)
 
 
 def scratch():
     v = lambda *shape, t=BF: pltpu.VMEM(shape, t)
-    pair = pltpu.SemaphoreType.DMA((320,))
     return [
+        v(2, 2, 128, 256), *[v(*a.shape, t=F32) for a in table_parts()],
         v(2, N, 512), v(QUARTER, N), v(QUARTER, N), v(N, QUARTER), v(N, QUARTER), v(512, 512),
         v(2, N, 128, t=F32), v(4, QUARTER, 256), v(2, 4, QUARTER, 128, t=F32),
         v(2, 2, 4, QUARTER, 128), v(2, 4, 128, 128), v(2, 4, 128, 128), v(2, 4, 128, 128),
@@ -629,20 +655,27 @@
         v(2, 128, 256, t=F32), v(2, 128, 256, t=F32),
         v(2, 1, 128, t=F32), v(2, 1, 128, t=F32), v(2, 16, 1, 128, t=F32), v(2, 4, 1, 128, t=F32),
         v(2, 1, 128, t=F32), v(2, 1, 128, t=F32),
-        pair, pair,
+        pltpu.SemaphoreType.DMA((SENDS,)), pltpu.SemaphoreType.DMA((RECEIVES,)),
+        pltpu.SemaphoreType.DMA((9,)),
     ]
+
+
+def hand_on(a, b, out, norms):
+    out[...] = a[...]
+    for i in range(2):
+        for j in range(2):
+            norms[i, j] = b[i, j]
 
 
 def per_device(traces, wavelet):
     vm = pl.BlockSpec(memory_space=pltpu.VMEM)
     sm = pl.BlockSpec(memory_space=pltpu.SMEM)
-    return pl.pallas_call(
+    hbm = pl.BlockSpec(memory_space=pl.ANY)
+    shapes = (jax.ShapeDtypeStruct((2, 2, 128, 256), F32), jax.ShapeDtypeStruct((2, 2), F32))
+    parts = pl.pallas_call(
         kernel,
-        out_shape=(
-            jax.ShapeDtypeStruct((2, 2, 128, 256), F32),
-            jax.ShapeDtypeStruct((2, 2), F32),
-        ),
-        in_specs=[vm, sm] + [vm] * 8,
+        out_shape=shapes,
+        in_specs=[hbm, sm] + [hbm] * 8,
         out_specs=(vm, sm),
         scratch_shapes=scratch(),
         compiler_params=pltpu.CompilerParams(
@@ -650,6 +683,9 @@
         ),
         name="whole",
     )(traces, wavelet, *table_parts())
+    return pl.pallas_call(
+        hand_on, out_shape=shapes, in_specs=[vm, sm], out_specs=(vm, sm), name="hand_on"
+    )(*parts)
 
 
 def solution(mesh):

time: 112 us -> 106 us (0.946)
  Pallas kernels: 109 us -> 105 us
  local copies, waits for them, and re-layouts: 2.44 us -> 0 us
    pallas_call x1 -> x2, Pallas kernels: 109 us -> 105 us  [the longest x1 103 us: per_device(): pl.pallas_call(kernel, out_shape=shapes, in_specs=[hbm, sm] + [hbm] * 8,...]
    unnamed x4 -> x0, local copies, waits for them, and re-layouts: 2.44 us -> none
where the time goes in v5:
time: 106 us
  Pallas kernels  105 us (99%)
    pallas_call x1, Pallas kernels, per_device(): pl.pallas_call(kernel, out_shape=shapes, in_specs=[hbm, sm] + [hbm] * 8,...  103 us

profile of v5, /device:TPU:1, one launch (start us, length us, event | category | flops | bytes accessed | tf_op | source)
XLA Modules:
  0.0 105.7 jit_solution(14516484504315980131)
XLA Ops:
  0.6 103.2 %whole.1 = (f32[2,2,128,256]{3,2,1,0:T(8,128)}, f32[2,2]{1,0:T(2,128)}) custom-call(bf16[2,2,128,256]{3,2,1,0:T(8,128)(2,1)} %tr_any.1, f32[2,2]{1,0:T(2,128)} %wave.1, f32[32,2048]{1,0:T(8,128)} %constant.16.clone.t0, f32[32,2048]{1,0:T(8,128)} %constant.17.clone.t1, f32[16,2048]{1,0:T(8,128)} %constant.18.clone.t2, f32[16,2048]{1,0:T(8,128)} %constant.19.clone.t3, ...), custom_call_target="tpu_custom_call" | custom-call | tf_op jit(solution)/shard_map/whole/pallas_call | solution.py:675
  103.8 1.9 %hand_on.1 = (f32[2,2,128,256]{3,2,1,0:T(8,128)}, f32[2,2]{1,0:T(2,128)}) custom-call(f32[2,2,128,256]{3,2,1,0:T(8,128)} %get-tuple-element.4.a, f32[2,2]{1,0:T(2,128)} %get-tuple-element.5.b), custom_call_target="tpu_custom_call" | custom-call | tf_op jit(solution)/shard_map/hand_on/pallas_call | solution.py:686

commit v6 on v5

--- a/solution.py
+++ b/solution.py
@@ -12,8 +12,8 @@
 MESH = pl.DeviceIdType.MESH
 N = 2048
 BASE = 32
-RECEIVES = 92
-SENDS = 16
+RECEIVES = 90
+SENDS = 14
 QUARTER = N // 4
 STEP = 0.4
 SHRINK = 0.2
@@ -42,7 +42,7 @@
     tr_any, wave, t0, t1, t2, t3, t4, t5, t6, t7, out, norms,
     tr, b0, b1, b2, b3, b4, b5, b6, b7,
     tf, tab_c, tab_s, inv_c, inv_s, perm, pg, ubt, tp, sb, ra, rb, qa, qb, dl, dr, ub, zt, xt,
-    trial, cfo, cb, hb, wt, hh, mb, mf, ot, nat, keep, got, st1, st2, sr1, sr2, nt, nr,
+    trial, cfo, cb, hb, wt, hh, mb, mf, ot, nat, keep, got, st1, sr1, nt, nr,
     ssem, rsem, lsem,
 ):
     tables_any = (t0, t1, t2, t3, t4, t5, t6, t7)
@@ -194,7 +194,7 @@
 
     def shift(at, axis, d):
         zz_, xx_ = at
-        return ((zz_ + d + 4) % 4, xx_) if axis == 0 else (zz_, (xx_ + d + 4) % 4)
+        return (zz_ + (1 - axis) * d + 4) % 4, (xx_ + axis * d + 4) % 4
 
     def neighbour(axis, d):
         a, b = shift((z, lane2), axis, d)
@@ -251,9 +251,12 @@
     mark("gather_a")
     home = (z, lane2)
     kinds = (0, 1, 2, 3)
-    first_axis = (0, 0, 0, 1)
-    first = [ag_start(home, first_axis[k], k) for k in kinds]
-    own = [ag_start(home, 1, k) for k in (0, 1, 2)]
+    first_axis = (0, 0, 1 - c, 1 - c)
+    first, own = {}, {}
+    for k in (0, 2, 1, 3):
+        first[k] = ag_start(home, first_axis[k], k)
+    for k in (0, 2, 1, 3):
+        own[k] = ag_start(home, 1 - first_axis[k], k)
     for copy in fetched[1:]:
         copy.wait()
     make_table(0, 16)
@@ -264,22 +267,16 @@
     def pass_on(k, hops):
         near[k, hops] = [ag_start(shift(home, first_axis[k], d), 1 - first_axis[k], k) for d in hops]
 
-    ag_forward(first[3])
-    for k in (0, 1, 2):
+    for k in (0, 2, 1, 3):
         ag_forward(first[k])
+    for k in (0, 2, 1, 3):
         pass_on(k, (-1, 1))
-        if k == 2:
-            own.append(ag_start(home, 0, 3))
         ag_forward(own[k])
-    pass_on(3, (-1, 1))
-    ag_finish(first[3])
-    for k in (0, 1, 2):
+    for k in (0, 2, 1, 3):
         ag_finish(first[k])
         pass_on(k, (2,))
-    pass_on(3, (2,))
-    ag_forward(own[3])
     mark("gather_c")
-    for k in kinds:
+    for k in (0, 2, 1, 3):
         for item in near[k, (-1, 1)]:
             ag_forward(item)
     for k in kinds:
@@ -288,7 +285,7 @@
     back_start()
     back_rows(z)
     mark("gather_d")
-    for k in kinds:
+    for k in (0, 2, 1, 3):
         ag_forward(near[k, (2,)][0])
     for k in kinds:
         for item in near[k, (-1, 1)]:
@@ -344,6 +341,9 @@
 
     offsets = [(a, b) for a in range(4) for b in range(4) if a or b]
     offsets.sort(key=lambda o: -(min(o[0], 4 - o[0]) + min(o[1], 4 - o[1])))
+
+    everyone = [(a, b, d) for a in range(4) for b in range(4) for d in range(4) if a or b or d]
+    everyone.sort(key=lambda o: -sum(min(i, 4 - i) for i in o))
 
     def place(a, b):
         return (z + a) % 4 * 4 + (lane2 + b) % 4
@@ -512,10 +512,9 @@
         lane = lax.broadcasted_iota(jnp.int32, (1, 128), 1)
         st1[it] = jnp.where(lane < 64, peak, squares)
         sid, sid_s = ids(1), out_id()
-        src_of = lambda q: st1.at[it]
-        dst_of = lambda q: sr1.at[it, q]
-        plane_exchange(src_of, dst_of, sid, sid_s)
-        sr1[it, p] = st1[it]
+        for k, (a, b, d) in enumerate(everyone):
+            send(st1.at[it], sr1.at[it, k], sid_s, sid, dev(place(a, b), (g + d) % 4))
+        sr1[it, 63] = st1[it]
         if it:
             mark("out_send")
             oid, oid_s = ids(1), out_id()
@@ -549,18 +548,9 @@
                 out_dst(p)[...] = out_src(p)[...]
 
             mark("stats_wait")
-        plane_wait(sr1.at[it, 0:15], sid, sid_s)
-        def joined(all_of):
-            return jnp.where(lane < 64, jnp.max(all_of, axis=0), jnp.sum(all_of, axis=0))
-
-        st2[it] = joined(sr1[it])
-        tid, tid_s = ids(1), out_id()
-        for d in (2, 1, 3):
-            send(st2.at[it], sr2.at[it, g], tid_s, tid, dev(p, (g + d) % 4))
-        sr2[it, g] = st2[it]
-        arrived(sr2.at[it, 0:3], tid)
-        sent(sr2.at[it, 0:3], tid_s)
-        both = joined(sr2[it])
+        plane_wait(sr1.at[it, 0:63], sid, sid_s)
+        found = sr1[it]
+        both = jnp.where(lane < 64, jnp.max(found, axis=0), jnp.sum(found, axis=0))
         totals.append(jnp.max(jnp.where(lane < 64, 0.0, both)))
         mark("shrink")
         level = SHRINK * jnp.max(jnp.where(lane < 64, both, 0.0))
@@ -653,7 +643,7 @@
         v(2, 32, N), v(2, 4, 128, 128), v(2, 4, 128, QUARTER), v(2, 128, N), v(2, 128, 512),
         v(2, 16, 32, 128, t=F32), v(2, 4, 128, 128, t=F32),
         v(2, 128, 256, t=F32), v(2, 128, 256, t=F32),
-        v(2, 1, 128, t=F32), v(2, 1, 128, t=F32), v(2, 16, 1, 128, t=F32), v(2, 4, 1, 128, t=F32),
+        v(2, 1, 128, t=F32), v(2, 64, 1, 128, t=F32),
         v(2, 1, 128, t=F32), v(2, 1, 128, t=F32),
         pltpu.SemaphoreType.DMA((SENDS,)), pltpu.SemaphoreType.DMA((RECEIVES,)),
         pltpu.SemaphoreType.DMA((9,)),

time: 106 us -> 109 us (1.028)
  Pallas kernels: 105 us -> 109 us
    pallas_call x1, Pallas kernels: 103 us -> 107 us  [per_device(): pl.pallas_call(kernel, out_shape=shapes, in_specs=[hbm, sm] + [hbm] * 8,...]
where the time goes in v6:
time: 109 us
  Pallas kernels  109 us (100%)
    pallas_call x1, Pallas kernels, per_device(): pl.pallas_call(kernel, out_shape=shapes, in_specs=[hbm, sm] + [hbm] * 8,...  107 us

profile of v6, /device:TPU:1, one launch (start us, length us, event | category | flops | bytes accessed | tf_op | source)
XLA Modules:
  0.0 109.3 jit_solution(4535248908317997740)
XLA Ops:
  0.6 106.8 %whole.1 = (f32[2,2,128,256]{3,2,1,0:T(8,128)}, f32[2,2]{1,0:T(2,128)}) custom-call(bf16[2,2,128,256]{3,2,1,0:T(8,128)(2,1)} %tr_any.1, f32[2,2]{1,0:T(2,128)} %wave.1, f32[32,2048]{1,0:T(8,128)} %constant.16.clone.t0, f32[32,2048]{1,0:T(8,128)} %constant.17.clone.t1, f32[16,2048]{1,0:T(8,128)} %constant.18.clone.t2, f32[16,2048]{1,0:T(8,128)} %constant.19.clone.t3, ...), custom_call_target="tpu_custom_call" | custom-call | tf_op jit(solution)/shard_map/whole/pallas_call | solution.py:665
  107.4 1.9 %hand_on.1 = (f32[2,2,128,256]{3,2,1,0:T(8,128)}, f32[2,2]{1,0:T(2,128)}) custom-call(f32[2,2,128,256]{3,2,1,0:T(8,128)} %get-tuple-element.4.a, f32[2,2]{1,0:T(2,128)} %get-tuple-element.5.b), custom_call_target="tpu_custom_call" | custom-call | tf_op jit(solution)/shard_map/hand_on/pallas_call | solution.py:676

commit v7 on v6

--- a/solution.py
+++ b/solution.py
@@ -251,7 +251,7 @@
     mark("gather_a")
     home = (z, lane2)
     kinds = (0, 1, 2, 3)
-    first_axis = (0, 0, 1 - c, 1 - c)
+    first_axis = (0, 0, 1, 0)
     first, own = {}, {}
     for k in (0, 2, 1, 3):
         first[k] = ag_start(home, first_axis[k], k)

time: 109 us -> 104 us (0.954)
  Pallas kernels: 109 us -> 103 us
    pallas_call x1, Pallas kernels: 107 us -> 101 us  [per_device(): pl.pallas_call(kernel, out_shape=shapes, in_specs=[hbm, sm] + [hbm] * 8,...]
where the time goes in v7:
time: 104 us
  Pallas kernels  103 us (99%)
    pallas_call x1, Pallas kernels, per_device(): pl.pallas_call(kernel, out_shape=shapes, in_specs=[hbm, sm] + [hbm] * 8,...  101 us

profile of v7, /device:TPU:1, one launch (start us, length us, event | category | flops | bytes accessed | tf_op | source)
XLA Modules:
  0.0 103.8 jit_solution(5718717514479316009)
XLA Ops:
  0.6 101.2 %whole.1 = (f32[2,2,128,256]{3,2,1,0:T(8,128)}, f32[2,2]{1,0:T(2,128)}) custom-call(bf16[2,2,128,256]{3,2,1,0:T(8,128)(2,1)} %tr_any.1, f32[2,2]{1,0:T(2,128)} %wave.1, f32[32,2048]{1,0:T(8,128)} %constant.16.clone.t0, f32[32,2048]{1,0:T(8,128)} %constant.17.clone.t1, f32[16,2048]{1,0:T(8,128)} %constant.18.clone.t2, f32[16,2048]{1,0:T(8,128)} %constant.19.clone.t3, ...), custom_call_target="tpu_custom_call" | custom-call | tf_op jit(solution)/shard_map/whole/pallas_call | solution.py:665
  101.9 1.9 %hand_on.1 = (f32[2,2,128,256]{3,2,1,0:T(8,128)}, f32[2,2]{1,0:T(2,128)}) custom-call(f32[2,2,128,256]{3,2,1,0:T(8,128)} %get-tuple-element.4.a, f32[2,2]{1,0:T(2,128)} %get-tuple-element.5.b), custom_call_target="tpu_custom_call" | custom-call | tf_op jit(solution)/shard_map/hand_on/pallas_call | solution.py:676

commit v8 on v7

--- a/solution.py
+++ b/solution.py
@@ -12,7 +12,7 @@
 MESH = pl.DeviceIdType.MESH
 N = 2048
 BASE = 32
-RECEIVES = 90
+RECEIVES = 102
 SENDS = 14
 QUARTER = N // 4
 STEP = 0.4
@@ -381,10 +381,10 @@
                 for r in range(4):
                     hh[part, r, :, ds(128 * g, 128, 128)] = wt[part, r].astype(F32).T.astype(BF)
             mark("g_gather")
-            gid, gid_s = ids(8), out_id()
+            gid, gid_s = ids(12), out_id()
 
             def held(gg, part, h=None):
-                which = slice(None) if h is None else pl.ds(2 * h, 2)
+                which = slice(None) if h is None else pl.ds(h, 1)
                 return hh.at[part, which, :, ds(128 * gg, 128, 128)]
 
             up, down, far = (g + 1) % 4, (g + 3) % 4, (g + 2) % 4
@@ -392,20 +392,20 @@
             def pass_held(gg, part, h, r_id, to):
                 send(held(gg, part, h), held(gg, part, h), gid_s, gid + r_id, dev(p, to))
 
-            for h in range(2):
+            for h in range(4):
                 pass_held(g, 0, h, h, up)
-                pass_held(g, 1, h, 2 + h, down)
-            pass_held(g, 1, None, 4, up)
-            pass_held(g, 0, None, 5, down)
-            for h in range(2):
+                pass_held(g, 1, h, 4 + h, down)
+            pass_held(g, 1, None, 8, up)
+            pass_held(g, 0, None, 9, down)
+            for h in range(4):
                 arrived(held(down, 0, h), gid + h)
-                pass_held(down, 0, h, 6, up)
-                arrived(held(up, 1, h), gid + 2 + h)
-                pass_held(up, 1, h, 7, down)
-            arrived(held(down, 1), gid + 4)
-            arrived(held(up, 0), gid + 5)
-            arrived(held(far, 0), gid + 6)
-            arrived(held(far, 1), gid + 7)
+                pass_held(down, 0, h, 10, up)
+                arrived(held(up, 1, h), gid + 4 + h)
+                pass_held(up, 1, h, 11, down)
+            arrived(held(down, 1), gid + 8)
+            arrived(held(up, 0), gid + 9)
+            arrived(held(far, 0), gid + 10)
+            arrived(held(far, 1), gid + 11)
             sent(hh.at[:, 0:3], gid_s)
 
             mark("g_right")
@@ -448,13 +448,11 @@
             lambda r, part: ubt.at[r, :, pl.ds(128 * part, 128)],
         )
         up, down, far = (g + 1) % 4, (g + 3) % 4, (g + 2) % 4
-        rid, rid_s = ids(6), out_id()
-
-        def piece(ref, gg, h, part):
-            return ref.at[it, part, pl.ds(2 * h, 2), ds(128 * gg, 128, 128), :]
-
-        def slot(ref, h, *part):
-            return ref.at[(it, *part, pl.ds(2 * h, 2))]
+        rid, rid_s = ids(10), out_id()
+
+        def piece(ref, gg, part, r=None):
+            which = slice(None) if r is None else pl.ds(r, 1)
+            return ref.at[it, part, which, ds(128 * gg, 128, 128), :]
 
         for r in range(4):
             there = pl.ds(r * QUARTER, QUARTER)
@@ -464,25 +462,22 @@
             tp[1, r] = ti_
             sb[it, 0, r] = tr_.astype(BF)
             sb[it, 1, r] = ti_.astype(BF)
-            if r % 2:
-                h = r // 2
-                send(piece(sb, far, h, 0), slot(ra, h), rid_s, rid + h, dev(p, up))
-                send(piece(sb, far, h, 1), slot(rb, h), rid_s, rid + 2 + h, dev(p, down))
+            send(piece(sb, far, 0, r), ra.at[it, pl.ds(r, 1)], rid_s, rid + r, dev(p, up))
+            send(piece(sb, far, 1, r), rb.at[it, pl.ds(r, 1)], rid_s, rid + 4 + r, dev(p, down))
 
         mark("scatter")
-        for h in range(2):
-            send(piece(sb, up, h, 1), slot(dl, h, 1), rid_s, rid + 4, dev(p, up))
-            send(piece(sb, down, h, 0), slot(dr, h, 0), rid_s, rid + 5, dev(p, down))
-        for h in range(2):
-            pair = pl.ds(2 * h, 2)
-            arrived(slot(ra, h), rid + h)
-            qa[it, pair] = (tp[0, pair, ds(128 * up, 128, 128), :] + ra[it, pair].astype(F32)).astype(BF)
-            send(slot(qa, h), slot(dl, h, 0), rid_s, rid + 4, dev(p, up))
-            arrived(slot(rb, h), rid + 2 + h)
-            qb[it, pair] = (tp[1, pair, ds(128 * down, 128, 128), :] + rb[it, pair].astype(F32)).astype(BF)
-            send(slot(qb, h), slot(dr, h, 1), rid_s, rid + 5, dev(p, down))
-        arrived(dl.at[it], rid + 4)
-        arrived(dr.at[it], rid + 5)
+        send(piece(sb, up, 1), dl.at[it, 1], rid_s, rid + 8, dev(p, up))
+        send(piece(sb, down, 0), dr.at[it, 0], rid_s, rid + 9, dev(p, down))
+        for r in range(4):
+            one = pl.ds(r, 1)
+            arrived(ra.at[it, one], rid + r)
+            qa[it, r] = (tp[0, r, ds(128 * up, 128, 128), :] + ra[it, r].astype(F32)).astype(BF)
+            send(qa.at[it, one], dl.at[it, 0, one], rid_s, rid + 8, dev(p, up))
+            arrived(rb.at[it, one], rid + 4 + r)
+            qb[it, r] = (tp[1, r, ds(128 * down, 128, 128), :] + rb[it, r].astype(F32)).astype(BF)
+            send(qb.at[it, one], dr.at[it, 1, one], rid_s, rid + 9, dev(p, down))
+        arrived(dl.at[it], rid + 8)
+        arrived(dr.at[it], rid + 9)
         sent(sb.at[it, :, 0:3], rid_s)
         total = tp[:, :, ds(128 * g, 128, 128), :] + dl[it].astype(F32)
         zt[it] = (total + dr[it].astype(F32)).astype(BF)
@@ -503,10 +498,13 @@
                 a, b = trial[0, r] + a, trial[1, r] + b
             trial[0, r] = a
             trial[1, r] = b
-            peaks.append(jnp.max(jnp.sqrt(a * a + b * b)))
+            v = a * a + b * b
+            v = jnp.maximum(jnp.maximum(v[:, :128], v[:, 128:256]), jnp.maximum(v[:, 256:384], v[:, 384:]))
+            peaks.append(v)
 
         forward(lambda part, q: xt[it, part, :, q * QUARTER : q * QUARTER + QUARTER].astype(F32), put_trial)
         peak = jnp.maximum(jnp.maximum(peaks[0], peaks[1]), jnp.maximum(peaks[2], peaks[3]))
+        peak = jnp.max(jnp.sqrt(peak))
 
         mark("stats")
         lane = lax.broadcasted_iota(jnp.int32, (1, 128), 1)
@@ -518,26 +516,29 @@
         if it:
             mark("out_send")
             oid, oid_s = ids(1), out_id()
-            for b in range(4):
-                v = [trial[part, r, :, 128 * b : 128 * b + 128] for r in range(4) for part in range(2)]
-                v = jnp.concatenate([jnp.concatenate(v[k::2], axis=1) for k in range(2)], axis=0)
+            away = jnp.logical_and(c == 1, x != y)
+            out_src = lambda q: cfo.at[:, :, ds(128 * q, 128, 128)]
+            out_dst = lambda q: ot.at[:, q]
+
+            def out_copy(q):
+                return rcopy(out_src(q), out_dst(p), oid_s, oid, chip(q // 4, q % 4, g, c))
+
+            order = perm[...]
+            for dz in (2, 1, 3, 0):
+                b = (z + dz) % 4
+                part_of = lambda part, r: trial[part, r, :, ds(128 * b, 128, 128)]
+                v = [jnp.concatenate([part_of(part, r) for r in range(4)], axis=1) for part in range(2)]
+                v = jnp.concatenate(v, axis=0)
                 hi = v.astype(BF)
                 rest = v - hi.astype(F32)
                 mid = rest.astype(BF)
                 low = (rest - mid.astype(F32)).astype(BF)
-                order = perm[...]
                 v = dot(hi, order) + dot(mid, order) + dot(low, order)
-                cfo[0, :, 512 * b : 512 * b + 512] = v[:32]
-                cfo[1, :, 512 * b : 512 * b + 512] = v[32:]
-            out_src = lambda q: cfo.at[:, :, ds(128 * q, 128, 128)]
-            out_dst = lambda q: ot.at[:, q]
-            away = jnp.logical_and(c == 1, x != y)
-
-            def out_copy(q):
-                return rcopy(out_src(q), out_dst(p), oid_s, oid, chip(q // 4, q % 4, g, c))
-
-            for a, b in offsets:
-                out_copy(place(a, b)).start()
+                cfo[0, :, ds(512 * b, 512, 512)] = v[:32]
+                cfo[1, :, ds(512 * b, 512, 512)] = v[32:]
+                for dx in (2, 1, 3, 0):
+                    if dz or dx:
+                        out_copy(place(dz, dx)).start()
 
             @pl.when(away)
             def _():

time: 104 us -> 103 us (level)
  no operation moved by 1% of the time
where the time goes in v8:
time: 103 us
  Pallas kernels  102 us (99%)
    pallas_call x1, Pallas kernels, per_device(): pl.pallas_call(kernel, out_shape=shapes, in_specs=[hbm, sm] + [hbm] * 8,...  100 us

profile of v8, /device:TPU:1, one launch (start us, length us, event | category | flops | bytes accessed | tf_op | source)
XLA Modules:
  0.0 102.9 jit_solution(11089988878973088453)
XLA Ops:
  0.6 100.3 %whole.1 = (f32[2,2,128,256]{3,2,1,0:T(8,128)}, f32[2,2]{1,0:T(2,128)}) custom-call(bf16[2,2,128,256]{3,2,1,0:T(8,128)(2,1)} %tr_any.1, f32[2,2]{1,0:T(2,128)} %wave.1, f32[32,2048]{1,0:T(8,128)} %constant.16.clone.t0, f32[32,2048]{1,0:T(8,128)} %constant.17.clone.t1, f32[16,2048]{1,0:T(8,128)} %constant.18.clone.t2, f32[16,2048]{1,0:T(8,128)} %constant.19.clone.t3, ...), custom_call_target="tpu_custom_call" | custom-call | tf_op jit(solution)/shard_map/whole/pallas_call | solution.py:666
  101.0 1.9 %hand_on.1 = (f32[2,2,128,256]{3,2,1,0:T(8,128)}, f32[2,2]{1,0:T(2,128)}) custom-call(f32[2,2,128,256]{3,2,1,0:T(8,128)} %get-tuple-element.4.a, f32[2,2]{1,0:T(2,128)} %get-tuple-element.5.b), custom_call_target="tpu_custom_call" | custom-call | tf_op jit(solution)/shard_map/hand_on/pallas_call | solution.py:677

commit v9 on v8

--- a/solution.py
+++ b/solution.py
@@ -12,7 +12,7 @@
 MESH = pl.DeviceIdType.MESH
 N = 2048
 BASE = 32
-RECEIVES = 102
+RECEIVES = 89
 SENDS = 14
 QUARTER = N // 4
 STEP = 0.4
@@ -208,23 +208,26 @@
 
     gather_s = out_id()
 
-    def ag_start(at, axis, half):
-        r_id = ids(3)
+    def ag_start(at, axis, half, done):
+        r_id = ids(2)
         send(block(at, half), block(at, half), gather_s, r_id, neighbour(axis, 1))
         send(block(at, half), block(at, half), gather_s, r_id + 1, neighbour(axis, -1))
-        return at, axis, half, r_id
+        return at, axis, half, r_id, done
 
     def ag_forward(item):
-        at, axis, half, r_id = item
+        at, axis, half, r_id, done = item
         left, right = shift(at, axis, -1), shift(at, axis, 1)
         arrived(block(left, half), r_id)
-        send(block(left, half, 0), block(left, half, 0), gather_s, r_id + 2, neighbour(axis, 1))
+        send(block(left, half, 0), block(left, half, 0), gather_s, done, neighbour(axis, 1))
         arrived(block(right, half), r_id + 1)
-        send(block(right, half, 1), block(right, half, 1), gather_s, r_id + 2, neighbour(axis, -1))
+        send(block(right, half, 1), block(right, half, 1), gather_s, done, neighbour(axis, -1))
 
     def ag_finish(item):
-        at, axis, half, r_id = item
-        arrived(block(shift(at, axis, 2), half), r_id + 2)
+        at, axis, half, r_id, done = item
+        arrived(block(shift(at, axis, 2), half), done)
+
+    def all_done(items, done):
+        arrived(tf.at[:, 0 : 32 * items, :], done)
 
     def make_table(first, last):
         @pl.loop(first, last)
@@ -254,9 +257,10 @@
     first_axis = (0, 0, 1, 0)
     first, own = {}, {}
     for k in (0, 2, 1, 3):
-        first[k] = ag_start(home, first_axis[k], k)
+        first[k] = ag_start(home, first_axis[k], k, ids(1))
+    own_done, near_done, far_done = ids(1), ids(1), ids(1)
     for k in (0, 2, 1, 3):
-        own[k] = ag_start(home, 1 - first_axis[k], k)
+        own[k] = ag_start(home, 1 - first_axis[k], k, own_done)
     for copy in fetched[1:]:
         copy.wait()
     make_table(0, 16)
@@ -265,7 +269,10 @@
     near = {}
 
     def pass_on(k, hops):
-        near[k, hops] = [ag_start(shift(home, first_axis[k], d), 1 - first_axis[k], k) for d in hops]
+        done = far_done if hops == (2,) else near_done
+        near[k, hops] = [
+            ag_start(shift(home, first_axis[k], d), 1 - first_axis[k], k, done) for d in hops
+        ]
 
     for k in (0, 2, 1, 3):
         ag_forward(first[k])
@@ -279,23 +286,19 @@
     for k in (0, 2, 1, 3):
         for item in near[k, (-1, 1)]:
             ag_forward(item)
-    for k in kinds:
-        ag_finish(own[k])
+    all_done(4, own_done)
     mark("gather_back")
     back_start()
     back_rows(z)
     mark("gather_d")
     for k in (0, 2, 1, 3):
         ag_forward(near[k, (2,)][0])
-    for k in kinds:
-        for item in near[k, (-1, 1)]:
-            ag_finish(item)
+    all_done(8, near_done)
     mark("gather_back")
     back_rows((z + 3) % 4)
     back_rows((z + 1) % 4)
     mark("gather_e")
-    for k in kinds:
-        ag_finish(near[k, (2,)][0])
+    all_done(4, far_done)
     sent(tf.at[:, 0:1920, :], gather_s)
     mark("gather_back")
     back_rows((z + 2) % 4)
@@ -662,6 +665,7 @@
     vm = pl.BlockSpec(memory_space=pltpu.VMEM)
     sm = pl.BlockSpec(memory_space=pltpu.SMEM)
     hbm = pl.BlockSpec(memory_space=pl.ANY)
+    block = pl.BlockSpec((1, 2, 128, 256), lambda i: (i, 0, 0, 0))
     shapes = (jax.ShapeDtypeStruct((2, 2, 128, 256), F32), jax.ShapeDtypeStruct((2, 2), F32))
     parts = pl.pallas_call(
         kernel,
@@ -675,7 +679,7 @@
         name="whole",
     )(traces, wavelet, *table_parts())
     return pl.pallas_call(
-        hand_on, out_shape=shapes, in_specs=[vm, sm], out_specs=(vm, sm), name="hand_on"
+        hand_on, out_shape=shapes, grid=(2,), in_specs=[block, sm], out_specs=(block, sm), name="hand_on"
     )(*parts)
 
 

time: 103 us -> 103 us (level)
  no operation moved by 1% of the time
where the time goes in v9:
time: 103 us
  Pallas kernels  102 us (99%)
    pallas_call x1, Pallas kernels, per_device(): pl.pallas_call(kernel, out_shape=shapes, in_specs=[hbm, sm] + [hbm] * 8,...  100 us

profile of v9, /device:TPU:1, one launch (start us, length us, event | category | flops | bytes accessed | tf_op | source)
XLA Modules:
  0.0 102.6 jit_solution(1737251723110212875)
XLA Ops:
  0.6 100.2 %whole.1 = (f32[2,2,128,256]{3,2,1,0:T(8,128)}, f32[2,2]{1,0:T(2,128)}) custom-call(bf16[2,2,128,256]{3,2,1,0:T(8,128)(2,1)} %tr_any.1, f32[2,2]{1,0:T(2,128)} %wave.1, f32[32,2048]{1,0:T(8,128)} %constant.16.clone.t0, f32[32,2048]{1,0:T(8,128)} %constant.17.clone.t1, f32[16,2048]{1,0:T(8,128)} %constant.18.clone.t2, f32[16,2048]{1,0:T(8,128)} %constant.19.clone.t3, ...), custom_call_target="tpu_custom_call" | custom-call | tf_op jit(solution)/shard_map/whole/pallas_call | solution.py:670
  100.9 1.8 %hand_on.1 = (f32[2,2,128,256]{3,2,1,0:T(8,128)}, f32[2,2]{1,0:T(2,128)}) custom-call(f32[2,2,128,256]{3,2,1,0:T(8,128)} %get-tuple-element.4.a, f32[2,2]{1,0:T(2,128)} %get-tuple-element.5.b), custom_call_target="tpu_custom_call" | custom-call | tf_op jit(solution)/shard_map/hand_on/pallas_call | solution.py:681

commit v10 on v9

--- a/solution.py
+++ b/solution.py
@@ -146,13 +146,13 @@
     to_second = rcopy(tr.at[1], landing, swap_s[1], swap + c, chip(z, y, x, 1))
     stays = jnp.logical_and(c == 1, x == y)
 
+    @pl.when(c == 1)
+    def _():
+        to_first.start()
+
     @pl.when(jnp.logical_not(stays))
     def _():
         to_second.start()
-
-    @pl.when(c == 1)
-    def _():
-        to_first.start()
 
     @pl.when(c == 0)
     def _():
@@ -599,7 +599,7 @@
 
     for part in range(2):
         keep[part] = turned(part, 1 - c)
-    send(keep, got, halves_s, halves, partner)
+        send(keep.at[part], got.at[part], halves_s, halves, partner)
     for part in range(2):
         out[c, part] = turned(part, c)
     mark("out_swap")

time: 103 us -> 103 us (level)
  no operation moved by 1% of the time
where the time goes in v10:
time: 103 us
  Pallas kernels  102 us (99%)
    pallas_call x1, Pallas kernels, per_device(): pl.pallas_call(kernel, out_shape=shapes, in_specs=[hbm, sm] + [hbm] * 8,...  100 us

profile of v10, /device:TPU:1, one launch (start us, length us, event | category | flops | bytes accessed | tf_op | source)
XLA Modules:
  0.0 102.6 jit_solution(12387223761285969298)
XLA Ops:
  0.6 100.1 %whole.1 = (f32[2,2,128,256]{3,2,1,0:T(8,128)}, f32[2,2]{1,0:T(2,128)}) custom-call(bf16[2,2,128,256]{3,2,1,0:T(8,128)(2,1)} %tr_any.1, f32[2,2]{1,0:T(2,128)} %wave.1, f32[32,2048]{1,0:T(8,128)} %constant.16.clone.t0, f32[32,2048]{1,0:T(8,128)} %constant.17.clone.t1, f32[16,2048]{1,0:T(8,128)} %constant.18.clone.t2, f32[16,2048]{1,0:T(8,128)} %constant.19.clone.t3, ...), custom_call_target="tpu_custom_call" | custom-call | tf_op jit(solution)/shard_map/whole/pallas_call | solution.py:670
  100.8 1.8 %hand_on.1 = (f32[2,2,128,256]{3,2,1,0:T(8,128)}, f32[2,2]{1,0:T(2,128)}) custom-call(f32[2,2,128,256]{3,2,1,0:T(8,128)} %get-tuple-element.4.a, f32[2,2]{1,0:T(2,128)} %get-tuple-element.5.b), custom_call_target="tpu_custom_call" | custom-call | tf_op jit(solution)/shard_map/hand_on/pallas_call | solution.py:681
